TPU v7x, 32 devices: a whole 2x2x4 slice. The times are simulated.
32 devices in a mesh: dp: 8 (over z, y), vocab: 4 (over x, core).
Axes of the slice: x: 2, y: 2, z: 4, core: 2. Of those that a mesh axis runs over, the one named last changes fastest.
Arguments:
- hidden_states: bfloat16 [4096, 2048], P('dp', 'vocab'), may hold values from -12 to 12
- teacher_logits: bfloat16 [4096, 16384], P('dp', 'vocab'), may hold values from -24 to 240
- head_weight: bfloat16 [2048, 16384], P(None, 'vocab'), as said below
Outputs:
- kl_per_token: float32 [4096], P('dp')
- hidden_grad: bfloat16 [4096, 2048], P('dp', 'vocab')
- head_grad: float32 [2048, 16384], P('dp', 'vocab')
Inputs may be any that keep to these rules, and one draw needn't show every extreme that they name: `head_weight`: every entry's magnitude is at most 18 / sqrt(2048).
All inputs are finite; a program needn't handle non-finite values.
Results may differ from a plain program's by a relative error of at most 0.014.
Values may be sent and summed in bfloat16 or wider, within the bound.
A program may use at most 128 MiB of HBM per device.

v0:
```python
import functools

import jax
import jax.numpy as jnp
from jax import lax
from jax.experimental import pallas as pl
from jax.experimental.pallas import tpu as pltpu
from jax.sharding import PartitionSpec as P

grad_scale = 8.0
PAIR = 2
MESH = pl.DeviceIdType.MESH


def slice_order(line):
    order = []
    low, high = 0, line - 1
    while low <= high:
        order.append(high)
        if low < high:
            order.append(low)
        low, high = low + 1, high - 1
    return order


def head_grad_kernel(
    line, chunks, width, rows, half,
    features_ref, grad_ref, out_ref,
    partner_grad, block, outgoing, incoming,
    pair_send, pair_recv, line_send, line_recv,
):
    me = lax.axis_index("dp")
    place = me // PAIR
    side = me - place * PAIR
    partner = place * PAIR + (PAIR - 1) - side
    has_down = place > 0
    has_up = place < line - 1
    up = jnp.where(has_up, me + PAIR, me)
    down = jnp.where(has_down, me - PAIR, me)

    barrier = pltpu.get_barrier_semaphore()
    pl.semaphore_signal(barrier, inc=1, device_id={"dp": partner}, device_id_type=MESH)

    @pl.when(has_down)
    def _():
        pl.semaphore_signal(barrier, inc=1, device_id={"dp": down}, device_id_type=MESH)

    @pl.when(has_up)
    def _():
        pl.semaphore_signal(barrier, inc=1, device_id={"dp": up}, device_id_type=MESH)

    pl.semaphore_wait(barrier, 1 + has_down.astype(jnp.int32) + has_up.astype(jnp.int32))

    def columns_of(chunk):
        return pl.ds(pl.multiple_of(chunk * width, width), width)

    def pair_copy(chunk):
        columns = columns_of(chunk)
        return pltpu.make_async_remote_copy(
            src_ref=grad_ref.at[:, columns],
            dst_ref=partner_grad.at[:, columns],
            send_sem=pair_send.at[chunk],
            recv_sem=pair_recv.at[chunk],
            device_id={"dp": partner},
            device_id_type=MESH,
        )

    def line_copy(chunk, part, slot, target):
        columns = columns_of(chunk)
        return pltpu.make_async_remote_copy(
            src_ref=outgoing.at[part, :, columns],
            dst_ref=incoming.at[slot, :, columns],
            send_sem=line_send.at[part, chunk],
            recv_sem=line_recv.at[slot, chunk],
            device_id={"dp": target},
            device_id_type=MESH,
        )

    ahead = min(3, chunks)
    window = min(2, chunks)

    @pl.loop(0, ahead)
    def _(chunk):
        pair_copy(chunk).start()

    def drain(chunk):
        for part in range(line):

            @pl.when(place < part)
            def _():
                line_copy(chunk, part, part, up).wait_send()

            @pl.when(place > part)
            def _():
                line_copy(chunk, part, part, down).wait_send()

    def forward(chunk, part, has_source, slot, target):
        columns = columns_of(chunk)

        @pl.when(has_source)
        def _():
            line_copy(chunk, part, part, target).wait_recv()
            outgoing[part, :, columns] = (
                block[...] + incoming[part, :, columns].astype(jnp.float32)
            ).astype(jnp.bfloat16)

        @pl.when(jnp.logical_not(has_source))
        def _():
            outgoing[part, :, columns] = block[...].astype(jnp.bfloat16)

        line_copy(chunk, part, slot, target).start()

    def finish(chunk):
        columns = columns_of(chunk)

        @pl.when(has_down)
        def _():
            line_copy(chunk, 0, place, down).wait_recv()
            out_ref[:, columns] += incoming[place, :, columns].astype(jnp.float32)

        @pl.when(has_up)
        def _():
            line_copy(chunk, 0, line, up).wait_recv()
            out_ref[:, columns] += incoming[line, :, columns].astype(jnp.float32)

    lag = min(2, chunks)

    @pl.loop(0, chunks)
    def _(chunk):
        pair_copy(chunk).wait_recv()

        @pl.when(chunk + ahead < chunks)
        def _():
            pair_copy(chunk + ahead).start()

        @pl.when(chunk >= window)
        def _():
            drain(chunk - window)

        columns = columns_of(chunk)
        for part in slice_order(line):
            begin = part * rows
            block[...] = jnp.dot(
                features_ref[begin : begin + rows, :half],
                grad_ref[:, columns],
                preferred_element_type=jnp.float32,
            ) + jnp.dot(
                features_ref[begin : begin + rows, half:],
                partner_grad[:, columns],
                preferred_element_type=jnp.float32,
            )

            @pl.when(place == part)
            def _():
                out_ref[:, columns] = block[...]

            @pl.when(place < part)
            def _():
                forward(chunk, part, has_down, part, up)

            @pl.when(place > part)
            def _():
                forward(chunk, part, has_up, jnp.where(place - 1 == part, line, part), down)

        @pl.when(chunk >= lag)
        def _():
            finish(chunk - lag)

    @pl.loop(chunks - lag, chunks)
    def _(chunk):
        finish(chunk)

    @pl.loop(chunks - window, chunks)
    def _(chunk):
        drain(chunk)

    @pl.loop(0, chunks)
    def _(chunk):
        pair_copy(chunk).wait_send()


def reduce_head_grad(features, logit_grad, shards):
    line = shards // PAIR
    rows = features.shape[0] // line
    half, local_vocab = logit_grad.shape
    width = 256
    chunks = local_vocab // width
    return pl.pallas_call(
        functools.partial(head_grad_kernel, line, chunks, width, rows, half),
        out_shape=jax.ShapeDtypeStruct((rows, local_vocab), jnp.float32),
        in_specs=[pl.BlockSpec(memory_space=pltpu.VMEM)] * 2,
        out_specs=pl.BlockSpec(memory_space=pltpu.VMEM),
        scratch_shapes=[
            pltpu.VMEM((half, local_vocab), jnp.bfloat16),
            pltpu.VMEM((rows, width), jnp.float32),
            pltpu.VMEM((line, rows, local_vocab), jnp.bfloat16),
            pltpu.VMEM((line + 1, rows, local_vocab), jnp.bfloat16),
            pltpu.SemaphoreType.DMA((chunks,)),
            pltpu.SemaphoreType.DMA((chunks,)),
            pltpu.SemaphoreType.DMA((line, chunks)),
            pltpu.SemaphoreType.DMA((line + 1, chunks)),
        ],
        compiler_params=pltpu.CompilerParams(collective_id=0, has_side_effects=True),
    )(features, logit_grad)


def per_device(shards, hidden_states, teacher_logits, head_weight):
    tokens = hidden_states.shape[0]
    model_width = head_weight.shape[0]
    line = shards // PAIR
    rows = model_width // shards
    side = lax.axis_index("dp") % PAIR

    gathered = lax.all_gather(hidden_states, "vocab", axis=1, tiled=True)

    def slices(parity):
        return jnp.concatenate(
            [
                lax.dynamic_slice_in_dim(gathered, (part * PAIR + parity) * rows, rows, axis=1)
                for part in range(line)
            ],
            axis=1,
        )

    kept, given = slices(side), slices(1 - side)
    swap = [(index, index + 1 - 2 * (index % PAIR)) for index in range(shards)]
    received = lax.ppermute(given, "dp", swap)

    student = jnp.dot(gathered, head_weight, preferred_element_type=jnp.float32)
    teacher = teacher_logits.astype(jnp.float32)
    student_top = jnp.max(student, axis=1)
    teacher_top = jnp.max(teacher, axis=1)
    teacher_terms = jnp.exp(teacher - teacher_top[:, None])
    stats = jnp.stack(
        [
            student_top,
            teacher_top,
            jnp.sum(jnp.exp(student - student_top[:, None]), axis=1),
            jnp.sum(teacher_terms, axis=1),
            jnp.sum(teacher_terms * (teacher - student), axis=1),
        ]
    )
    stats, received = lax.optimization_barrier((stats, received))
    stats = lax.all_gather(stats, "vocab", axis=0, tiled=False)
    features = jnp.concatenate([kept.T, received.T], axis=1)
    student_max = jnp.max(stats[:, 0], axis=0)
    teacher_max = jnp.max(stats[:, 1], axis=0)
    student_scale = jnp.exp(stats[:, 0] - student_max)
    teacher_scale = jnp.exp(stats[:, 1] - teacher_max)
    student_total = jnp.sum(stats[:, 2] * student_scale, axis=0)
    teacher_total = jnp.sum(stats[:, 3] * teacher_scale, axis=0)
    cross_term = jnp.sum(stats[:, 4] * teacher_scale, axis=0)
    student_log = student_max + jnp.log(student_total)
    teacher_log = teacher_max + jnp.log(teacher_total)
    divergence = cross_term / teacher_total - teacher_log + student_log
    logit_grad = (
        grad_scale
        * (jnp.exp(student - student_log[:, None]) - jnp.exp(teacher - teacher_log[:, None]))
    ).astype(jnp.bfloat16)
    logit_grad, features = lax.optimization_barrier((logit_grad, features))
    partial_value = lax.dot_general(
        logit_grad, head_weight, (((1,), (1,)), ((), ())), preferred_element_type=jnp.float32
    ).astype(jnp.bfloat16)
    partial_value, logit_grad = lax.optimization_barrier((partial_value, logit_grad))
    hidden_grad = lax.psum_scatter(partial_value, "vocab", scatter_dimension=1, tiled=True)
    head_grad = reduce_head_grad(features, logit_grad, shards)
    return (divergence, hidden_grad, head_grad)


def solution(mesh):
    in_specs = (P("dp", "vocab"), P("dp", "vocab"), P(None, "vocab"))
    out_specs = (P("dp"), P("dp", "vocab"), P("dp", "vocab"))
    return jax.shard_map(
        functools.partial(per_device, mesh.shape["dp"]),
        mesh=mesh, in_specs=in_specs, out_specs=out_specs, check_vma=False,
    )
```

profile of v0, /device:TPU:0, one launch (start us, length us, event | category | flops | bytes accessed | tf_op | source)
XLA Modules:
  0.0 300.2 jit_solution(12785606905717433119)
XLA Ops:
  7.2 0.0 all-gather.4.cloned.1.call-start
  7.2 2.0 copy.10
  9.3 0.0 all-gather.4.cloned.1.call-update
  9.3 0.0 reduce-scatter.2.cloned.1.call-start
  9.4 2.8 reduce_max.46
  12.2 23.2 %all-gather.4.cloned.1.call-done = bf16[512,2048]{0,1:T(8,128)(2,1)} async-done(((bf16[512,512]{0,1:T(8,128)(2,1)}), bf16[512,2048]{0,1:T(8,128)(2,1)}) %all-gather.4.cloned.1.call-update) | async-done | bytes 2097168 | tf_op jit(solution)/shard_map/all_gather | solution.py:214
  35.4 0.0 copy-start.4
  35.4 1.9 constant_dynamic-slice_fusion.3
  37.3 0.1 pad_maximum_fusion.1
  37.4 0.0 copy-start
  37.4 1.5 collective-permute-start
  38.9 0.0 copy-done.4
  38.9 11.9 %fusion.16 = (f32[512]{0:T(512)S(1)}, f32[512,4096]{1,0:T(8,128)S(1)}) fusion(bf16[512,2048]{0,1:T(8,128)(2,1)S(1)} %copy-done.4, bf16[2048,4096]{1,0:T(8,128)(2,1)} %param.5), kind=kOutput, calls=%fused_computation.42 | convolution fusion | flops 8592031744 | bytes 27265024 | tf_op jit(solution)/shard_map/dot_general | solution.py:229
  50.9 0.0 copy-start.2
  50.9 0.0 copy-done
  50.9 3.9 %fusion.3 = (f32[512]{0:T(512)S(1)}, f32[512]{0:T(512)S(1)}, f32[512]{0:T(512)S(1)}) fusion(bf16[512,4096]{1,0:T(8,128)(2,1)S(1)} %copy-done, f32[512,4096]{1,0:T(8,128)S(1)} %get-tuple-element.39, f32[512]{0:T(512)S(1)} %reduce_max.52, f32[512]{0:T(512)S(1)} %get-tuple-element.38), kind=kLoop, calls=%fused_computation.6 | loop fusion | flops 16775680 | bytes 12593152 | tf_op jit(solution)/shard_map/reduce_sum | solution.py:240
  54.8 0.0 copy-done.2
  54.8 0.0 copy-start.1
  54.8 0.1 maximum_bitcast_fusion
  54.9 7.8 %collective-permute-done = bf16[512,1024]{0,1:T(8,128)(2,1)S(1)} collective-permute-done((bf16[512,1024]{0,1:T(8,128)(2,1)S(1)}, bf16[512,1024]{0,1:T(8,128)(2,1)S(1)}, u32[]{:S(2)}, u32[]{:S(2)}) %collective-permute-start) | collective-permute-done | bytes 1048608 | tf_op jit(solution)/shard_map/ppermute | solution.py:227
  62.8 5.2 %all-gather.1 = f32[4,5,512]{2,1,0:T(8,128)S(1)} all-gather(f32[1,5,512]{2,1,0:T(8,128)S(1)} %bitcast.46), channel_id=2, replica_groups=mesh['dp'=8,'vocab'=4] {'vocab'}, dimensions={0}, use_global_device_ids=true | all-gather | bytes 51200 | tf_op jit(solution)/shard_map/all_gather | solution.py:244
  68.0 1.7 pad_maximum_fusion.features_ref
  69.7 0.6 subtract_add_fusion
  70.3 0.0 copy-done.1
  70.3 5.4 %fusion.7.grad_ref = bf16[512,4096]{1,0:T(8,128)(2,1)S(1)} fusion(bf16[512,4096]{1,0:T(8,128)(2,1)S(1)} %copy-done.1, f32[512,4096]{1,0:T(8,128)} %copy-done.2, f32[512]{0:T(512)S(1)} %get-tuple-element.23, f32[512]{0:T(512)S(1)} %get-tuple-element.24), kind=kLoop, calls=%fused_computation.10 | loop fusion | flops 12582912 | bytes 16781312 | tf_op jit(solution)/shard_map/convert_element_type | solution.py:259
  75.7 0.0 copy-start.3
  75.7 2.0 copy-done.3
  77.7 13.4 %convolution_convert_fusion = bf16[512,2048]{1,0:T(8,128)(2,1)} fusion(bf16[512,4096]{1,0:T(8,128)(2,1)S(1)} %fusion.7.grad_ref, bf16[2048,4096]{1,0:T(8,128)(2,1)} %param.5), kind=kOutput, calls=%fused_computation.12 | convolution fusion | flops 8590983168 | bytes 23068672 | tf_op jit(solution)/shard_map/dot_general | solution.py:261
  91.2 0.0 reduce-scatter.2.cloned.1.call-update
  91.2 197.5 %shard_map.58 = f32[256,4096]{1,0:T(8,128)} custom-call(bf16[1024,1024]{1,0:T(8,128)(2,1)} %pad_maximum_fusion.features_ref, bf16[512,4096]{1,0:T(8,128)(2,1)} %copy-done.3), custom_call_target="tpu_custom_call" | custom-call | tf_op jit(solution)/shard_map/pallas_call | solution.py:188
  288.7 0.0 reduce-scatter.2.cloned.1.call-done
  288.7 4.7 %copy.42 = f32[256,4096]{1,0:T(8,128)} copy(f32[256,4096]{1,0:T(8,128)} %shard_map.58) | data formatting | bytes 8388608
  (4 shorter events, 0.1 us)
Async XLA Ops:
  7.2 28.3 %all-gather.4.cloned.1.call-start = ((), (), s32[]{:S(2)}) async-start(), calls=%async_computation.1 | async-start | bytes 2621440 | tf_op jit(solution)/shard_map/all_gather | solution.py:214
  9.3 279.4 %reduce-scatter.2.cloned.1.call-start = ((), (), s32[]{:S(2)}) async-start(), calls=%async_computation.2 | async-start | bytes 2621440 | tf_op jit(solution)/shard_map/reduce_scatter | solution.py:265
  35.4 3.5 %copy-start.4 = (bf16[512,2048]{0,1:T(8,128)(2,1)S(1)}, bf16[512,2048]{0,1:T(8,128)(2,1)}, u32[]{:S(2)}) copy-start(bf16[512,2048]{0,1:T(8,128)(2,1)} %all-gather.4.cloned.1.call-done) | copy-start | bytes 6291460
  37.4 13.5 %copy-start = (bf16[512,4096]{1,0:T(8,128)(2,1)S(1)}, bf16[512,4096]{1,0:T(8,128)(2,1)}, u32[]{:S(2)}) copy-start(bf16[512,4096]{1,0:T(8,128)(2,1)} %param.4) | copy-start | bytes 12582916
  37.4 25.4 %collective-permute-start = (bf16[512,1024]{0,1:T(8,128)(2,1)S(1)}, bf16[512,1024]{0,1:T(8,128)(2,1)S(1)}, u32[]{:S(2)}, u32[]{:S(2)}) collective-permute-start(bf16[512,1024]{0,1:T(8,128)(2,1)S(1)} %pad_maximum_fusion.1), channel_id=1, source_target_pairs={{0,4},{4,0},{8,12},{12,8},{16,20},{20,16},{24,28},{28,24},{1,5},{5... | collective-permute-start | bytes 3145736 | tf_op jit(solution)/shard_map/ppermute | solution.py:227
  50.9 3.9 %copy-start.2 = (f32[512,4096]{1,0:T(8,128)}, f32[512,4096]{1,0:T(8,128)S(1)}, u32[]{:S(2)}) copy-start(f32[512,4096]{1,0:T(8,128)S(1)} %get-tuple-element.39) | copy-start | bytes 25165828
  54.8 15.5 %copy-start.1 = (bf16[512,4096]{1,0:T(8,128)(2,1)S(1)}, bf16[512,4096]{1,0:T(8,128)(2,1)}, u32[]{:S(2)}) copy-start(bf16[512,4096]{1,0:T(8,128)(2,1)} %param.4) | copy-start | bytes 12582916
  75.7 2.0 copy-start.3
Sparse Core Ops, SparseCore 0:
  10.1 25.2 all-gather.3
  91.3 31.1 reduce-scatter.1
where the time goes:
time: 300 us
  Pallas kernels  197 us (66%)
  waiting for transfers between devices  31.1 us (10%)
  matrix products  25.4 us (8%)
  other arithmetic  14.6 us (5%)
  between operations  14.2 us (5%)
  local copies, waits for them, and re-layouts  10.6 us (4%)
  blocking collectives  5.22 us (2%)
    pallas_call x1, Pallas kernels, reduce_head_grad(): pl.pallas_call(functools.partial(head_grad_kernel, line, chunks, width, r...  197 us
    all_gather x1, waiting for transfers between devices, per_device(): gathered = lax.all_gather(hidden_states, 'vocab', axis=1, tiled=True)  23.2 us
    dot_general x1, matrix products, per_device(): lax.dot_general(logit_grad, head_weight, (((1,), (1,)), ((), ())), prefer...  13.4 us
    dot_general x1, matrix products, per_device(): student = jnp.dot(gathered, head_weight, preferred_element_type=jnp.float32)  11.9 us
    unnamed x12, local copies, waits for them, and re-layouts  8.73 us
    ppermute x1, waiting for transfers between devices, per_device(): received = lax.ppermute(given, 'dp', swap)  7.83 us
  transfers between devices with their start and end apart: 3, of which 2 were waited for; matrix products, arithmetic and copies ran while one was open for 6% of the time, Pallas kernels for 66%

commit v1 on v0

v1 whole, which is shorter than its diff:
```python
import functools

import jax
import jax.numpy as jnp
from jax import lax
from jax.experimental import pallas as pl
from jax.experimental.pallas import tpu as pltpu
from jax.sharding import PartitionSpec as P

grad_scale = 8.0
PAIR = 2
CORES = 2
LANES = 128
MESH = pl.DeviceIdType.MESH
f32 = jnp.float32
bf16 = jnp.bfloat16


class Plan:
    def __init__(self, shards, vocab, tokens, shard, model_width, columns):
        self.line = shards // PAIR
        self.vocab = vocab
        self.chips = vocab // CORES
        self.tokens = tokens
        self.shard = shard
        self.model_width = model_width
        self.columns = columns
        self.halves = 2
        self.half_tokens = tokens // self.halves
        self.half = columns // PAIR
        self.width = min(256, self.half)
        self.chunks = self.half // self.width
        self.rows2 = model_width // self.line
        self.rows = self.rows2 // PAIR
        self.window = min(3, self.chunks)
        self.lag = min(2, self.chunks)
        self.end_lag = self.lag + 2
        self.last_lag = self.end_lag + 1
        self.ahead = min(2, self.chunks)
        self.hid_width = min(256, shard)
        self.hid_subs = shard // self.hid_width
        self.hid_blocks = vocab * self.hid_subs
        self.slots = 2 if self.line == 4 else self.line + 1


def fused_kernel(
    plan,
    hidden_ref, teacher_ref, weight_ref,
    kl_ref, hid_ref, out_ref,
    weight, student, grad, gathered, features, pair_grad, incoming, outgoing, block,
    pair_out, pair_in, hid_out, hid_in, hid_far_out, hid_far_in, hid_sum,
    row_student, row_teacher, lane_stats, stats,
    load_sem, weight_sem, out_sem,
    gather_send, gather_recv, fy_send, fy_recv, fz_send, fz_recv, fx_send, fx_recv, fc_send, fc_recv,
    stat_send, stat_recv, y_send, y_recv, zo_send, zo_recv, zf_send, zf_recv,
    line_send, line_recv, last_send, last_recv,
    hc_send, hc_recv, hx_send, hx_recv,
):
    line, vocab, chips = plan.line, plan.vocab, plan.chips
    tokens, shard, half, width, chunks = plan.tokens, plan.shard, plan.half, plan.width, plan.chunks
    rows2, rows, half_tokens = plan.rows2, plan.rows, plan.half_tokens
    columns = plan.columns

    me = lax.axis_index("dp")
    v = lax.axis_index("vocab")
    place = me // PAIR
    side = me - place * PAIR
    partner = place * PAIR + (PAIR - 1) - side
    chip = v // CORES
    core = v - chip * CORES
    other_core = chip * CORES + (CORES - 1) - core
    has_down = place > 0
    has_up = place < line - 1
    up = jnp.where(has_up, me + PAIR, me)
    down = jnp.where(has_down, me - PAIR, me)
    is_low = place == 0
    is_high = place == line - 1
    is_end = jnp.logical_or(is_low, is_high)
    next_low = place == 1
    next_high = place == line - 2
    is_next = jnp.logical_or(next_low, next_high)
    inner = jnp.where(is_low, up, down)

    def chip_after(step):
        return lax.rem(chip + step, chips)

    def chip_before(step):
        return lax.rem(chip + chips - step, chips)

    def shard_of(index):
        return pl.ds(pl.multiple_of(index * shard, shard), shard)

    def chip_rows(index):
        return pl.ds(pl.multiple_of(index * CORES * shard, CORES * shard), CORES * shard)

    def token_half(part):
        return pl.ds(part * half_tokens, half_tokens)

    def columns_of(chunk):
        return pl.ds(pl.multiple_of(chunk * width, width), width)

    def grad_columns(which, chunk):
        return pl.ds(pl.multiple_of(which * half + chunk * width, width), width)

    def remote(src, dst, send, recv, **target):
        return pltpu.make_async_remote_copy(
            src_ref=src, dst_ref=dst, send_sem=send, recv_sem=recv, device_id=target, device_id_type=MESH
        )

    own_load = pltpu.make_async_copy(hidden_ref, gathered.at[:, shard_of(v)], load_sem.at[0])
    teacher_load = pltpu.make_async_copy(teacher_ref, grad, load_sem.at[1])

    def weight_load(step):
        part = chip_rows(chip_before(step))
        return pltpu.make_async_copy(weight_ref.at[part, :], weight.at[part, :], weight_sem.at[step])

    barrier = pltpu.get_barrier_semaphore()
    for step in range(1, vocab):
        pl.semaphore_signal(
            barrier, inc=1, device_id={"vocab": lax.rem(v + step, vocab)}, device_id_type=MESH
        )
    pl.semaphore_signal(barrier, inc=1, device_id={"dp": partner}, device_id_type=MESH)

    @pl.when(has_down)
    def _():
        pl.semaphore_signal(barrier, inc=1, device_id={"dp": down}, device_id_type=MESH)

    @pl.when(has_up)
    def _():
        pl.semaphore_signal(barrier, inc=1, device_id={"dp": up}, device_id_type=MESH)

    own_load.start()
    weight_load(0).start()
    teacher_load.start()
    for step in range(1, chips):
        weight_load(step).start()
    own_load.wait()
    pl.semaphore_wait(barrier, vocab + has_down.astype(jnp.int32) + has_up.astype(jnp.int32))

    def gather_copy(index, part, column, target):
        ref = gathered.at[token_half(part), shard_of(column)]
        return remote(ref, ref, gather_send.at[index, part], gather_recv.at[index, part], vocab=target)

    def gather_far(step, part):
        return gather_copy(step, part, v, chip_after(step) * CORES + core)

    def gather_pass(step, part):
        return gather_copy(chips - 1 + step, part, chip_before(step) * CORES + core, other_core)

    for part in range(plan.halves):
        for step in range(1, chips):
            gather_far(step, part).start()
        gather_copy(0, part, v, other_core).start()

    def set_ref(which, index):
        return features.at[shard_of(index), pl.ds(which * tokens, tokens)]

    def turn(index):
        features[shard_of(index), 0:tokens] = gathered[:, shard_of(index)].T

    def feature_y(step):
        index = chip_before(step) * CORES + core
        return remote(set_ref(0, index), set_ref(1, index), fy_send.at[step], fy_recv.at[step], dp=partner)

    def feature_z(which):
        return remote(set_ref(which, v), set_ref(2 + which, v), fz_send.at[which], fz_recv.at[which], dp=inner)

    def feature_x(which, step):
        ref = set_ref(which, v)
        return remote(
            ref, ref, fx_send.at[which - 2, step], fx_recv.at[which - 2, step],
            vocab=chip_after(step) * CORES + core,
        )

    def feature_core(which, step):
        ref = set_ref(which, chip_before(step) * CORES + core)
        return remote(ref, ref, fc_send.at[which - 1, step], fc_recv.at[which - 1, step], vocab=other_core)

    turn(v)
    feature_y(0).start()

    @pl.when(is_end)
    def _():
        feature_z(0).start()

    for part in range(plan.halves):
        gather_copy(0, part, other_core, other_core).wait_recv()
    weight_load(0).wait()
    dot_width = min(512, columns)

    @pl.loop(0, columns // dot_width)
    def _(index):
        where = pl.ds(pl.multiple_of(index * dot_width, dot_width), dot_width)
        student[:, where] = jnp.dot(
            gathered[:, chip_rows(chip)], weight[chip_rows(chip), where], preferred_element_type=f32
        )

    teacher_load.wait()
    band = 32

    @pl.loop(0, tokens // band)
    def _(index):
        where = pl.ds(pl.multiple_of(index * band, band), band)
        top = grad[where, 0:LANES]
        for column in range(1, columns // LANES):
            top = jnp.maximum(top, grad[where, column * LANES : (column + 1) * LANES])
        lane_stats[0, where, :] = top.astype(f32)

    row_teacher[...] = jnp.broadcast_to(jnp.max(lane_stats[0], axis=1, keepdims=True), (tokens, LANES))
    turn(other_core)

    def stat_copy(step, part, owner, target):
        ref = stats.at[owner, :, token_half(part)]
        return remote(ref, ref, stat_send.at[step, part], stat_recv.at[step, part], vocab=target)

    def first_half(part):
        where_rows = token_half(part)
        for step in range(1, chips):
            gather_copy(step, part, chip_before(step) * CORES + core, other_core).wait_recv()
            gather_pass(step, part).start()
        for step in range(1, chips):
            gather_copy(
                chips - 1 + step, part, chip_before(step) * CORES + (CORES - 1) - core, other_core
            ).wait_recv()
        if part == 0:
            for step in range(1, chips):
                weight_load(step).wait()
        lane_stats[0, where_rows, :] = jnp.full((half_tokens, LANES), -jnp.inf, f32)

        @pl.loop(0, columns // dot_width)
        def _(index):
            where = pl.ds(pl.multiple_of(index * dot_width, dot_width), dot_width)
            total = student[where_rows, where]
            for step in range(1, chips):
                far = chip_rows(chip_before(step))
                total = total + jnp.dot(
                    gathered[where_rows, far], weight[far, where], preferred_element_type=f32
                )
            student[where_rows, where] = total
            top = lane_stats[0, where_rows, :]
            for column in range(dot_width // LANES):
                top = jnp.maximum(top, total[:, column * LANES : (column + 1) * LANES])
            lane_stats[0, where_rows, :] = top

        student_top = jnp.max(lane_stats[0, where_rows, :], axis=1, keepdims=True)
        row_student[where_rows, :] = jnp.broadcast_to(student_top, (half_tokens, LANES))

        @pl.loop(0, half_tokens // band)
        def _(index):
            where = pl.ds(pl.multiple_of(part * half_tokens + index * band, band), band)
            student_max, teacher_max = row_student[where, :], row_teacher[where, :]
            sums = [jnp.zeros((band, LANES), f32) for _ in range(3)]
            for column in range(columns // LANES):
                lanes = slice(column * LANES, (column + 1) * LANES)
                logit, target = student[where, lanes], grad[where, lanes].astype(f32)
                term = jnp.exp(target - teacher_max)
                sums[0] += jnp.exp(logit - student_max)
                sums[1] += term
                sums[2] += term * (target - logit)
            for which in range(3):
                lane_stats[which, where, :] = sums[which]

        lane = lax.broadcasted_iota(jnp.int32, (half_tokens, LANES), 1)
        packed = jnp.where(lane == 0, row_student[where_rows, :], row_teacher[where_rows, :])
        for which in range(3):
            total = jnp.sum(lane_stats[which, where_rows, :], axis=1, keepdims=True)
            packed = jnp.where(lane == 2 + which, jnp.broadcast_to(total, packed.shape), packed)
        stats[v, :, where_rows] = packed.T[0:8, :]
        for step in range(1, vocab):
            stat_copy(step, part, v, lax.rem(v + step, vocab)).start()

    def y_copy(part, chunk):
        return remote(
            grad.at[token_half(part), grad_columns(PAIR - 1 - side, chunk)],
            pair_grad.at[token_half(part), columns_of(chunk)],
            y_send.at[part, chunk], y_recv.at[part, chunk], dp=partner,
        )

    def end_own(part, chunk):
        return remote(
            grad.at[token_half(part), grad_columns(side, chunk)],
            pair_grad.at[pl.ds(tokens + part * half_tokens, half_tokens), columns_of(chunk)],
            zo_send.at[part, chunk], zo_recv.at[part, chunk], dp=inner,
        )

    def end_pair(part, chunk):
        return remote(
            pair_grad.at[token_half(part), columns_of(chunk)],
            pair_grad.at[pl.ds(2 * tokens + part * half_tokens, half_tokens), columns_of(chunk)],
            zf_send.at[part, chunk], zf_recv.at[part, chunk], dp=inner,
        )

    def second_half(part):
        where_rows = token_half(part)
        for step in range(1, vocab):
            stat_copy(step, part, lax.rem(v + vocab - step, vocab), other_core).wait_recv()
        parts = [stats[index, :, where_rows] for index in range(vocab)]
        student_max = functools.reduce(jnp.maximum, [p[0:1] for p in parts])
        teacher_max = functools.reduce(jnp.maximum, [p[1:2] for p in parts])
        student_total = sum(p[2:3] * jnp.exp(p[0:1] - student_max) for p in parts)
        teacher_scales = [jnp.exp(p[1:2] - teacher_max) for p in parts]
        teacher_total = sum(p[3:4] * scale for p, scale in zip(parts, teacher_scales))
        cross = sum(p[4:5] * scale for p, scale in zip(parts, teacher_scales))
        student_log = student_max + jnp.log(student_total)
        teacher_log = teacher_max + jnp.log(teacher_total)
        kl_ref[:, where_rows] = cross / teacher_total - teacher_log + student_log
        row = lax.broadcasted_iota(jnp.int32, (LANES, half_tokens), 0)
        packed = jnp.where(
            row == 0,
            jnp.broadcast_to(student_log, (LANES, half_tokens)),
            jnp.broadcast_to(teacher_log, (LANES, half_tokens)),
        ).T
        row_student[where_rows, :] = jnp.broadcast_to(packed[:, 0:1], (half_tokens, LANES))
        row_teacher[where_rows, :] = jnp.broadcast_to(packed[:, 1:2], (half_tokens, LANES))

        @pl.loop(0, half_tokens // band)
        def _(index):
            where = pl.ds(pl.multiple_of(part * half_tokens + index * band, band), band)
            student_row, teacher_row = row_student[where, :], row_teacher[where, :]
            for column in range(columns // LANES):
                lanes = slice(column * LANES, (column + 1) * LANES)
                value = jnp.exp(student[where, lanes] - student_row) - jnp.exp(
                    grad[where, lanes].astype(f32) - teacher_row
                )
                grad[where, lanes] = (grad_scale * value).astype(bf16)

        @pl.loop(0, chunks)
        def _(chunk):
            y_copy(part, chunk).start()

        @pl.when(is_end)
        def _():
            for chunk in range(plan.ahead):
                end_own(part, chunk).start()

    def first_service():
        feature_y(0).wait_recv()
        feature_core(1, 0).start()

        @pl.when(is_end)
        def _():
            feature_z(1).start()

        @pl.when(is_next)
        def _():
            feature_z(0).wait_recv()
            for step in range(1, chips):
                feature_x(2, step).start()
            feature_core(2, 0).start()

        for step in range(1, chips):
            turn(chip_before(step) * CORES + core)
            feature_y(step).start()
        for step in range(1, chips):
            turn(chip_before(step) * CORES + (CORES - 1) - core)

    def second_service():
        for step in range(1, chips):
            feature_y(step).wait_recv()
            feature_core(1, step).start()

        @pl.when(is_next)
        def _():
            feature_z(1).wait_recv()
            for step in range(1, chips):
                feature_x(3, step).start()
            feature_core(3, 0).start()
            for which in (2, 3):
                for step in range(1, chips):
                    feature_x(which, step).wait_recv()
                    feature_core(which, step).start()
            for which in (2, 3):
                for step in range(chips):
                    feature_core(which, step).wait_recv()

        for step in range(chips):
            feature_core(1, step).wait_recv()

    first_half(0)
    first_half(1)
    second_half(0)
    first_service()
    second_half(1)
    second_service()

    def hid_core(index):
        return remote(
            hid_out.at[index], hid_in.at[index], hc_send.at[index], hc_recv.at[index], vocab=other_core
        )

    def hid_far(index):
        return remote(
            hid_far_out.at[index], hid_far_in.at[index], hx_send.at[index], hx_recv.at[index],
            vocab=lax.rem(chip + 1 + index, chips) * CORES + core,
        )

    def hid_block(index):
        piece = index // plan.hid_subs
        sub = index - piece * plan.hid_subs
        mine = piece >= chips
        order = jnp.where(mine, piece - chips, piece)
        target = lax.rem(chip + 1 + order, chips) * CORES + jnp.where(mine, core, (CORES - 1) - core)
        where = pl.ds(pl.multiple_of(target * shard + sub * plan.hid_width, plan.hid_width), plan.hid_width)
        lanes = pl.ds(pl.multiple_of(sub * plan.hid_width, plan.hid_width), plan.hid_width)
        last_sub = sub == plan.hid_subs - 1
        value = lax.dot_general(
            grad[...], weight[where, :], (((1,), (1,)), ((), ())), preferred_element_type=f32
        )

        @pl.when(jnp.logical_not(mine))
        def _():
            hid_out[order, :, lanes] = value.astype(bf16)

            @pl.when(last_sub)
            def _():
                hid_core(order).start()

        @pl.when(mine)
        def _():
            @pl.when(sub == 0)
            def _():
                hid_core(order).wait_recv()

            total = value + hid_in[order, :, lanes].astype(f32)

            @pl.when(order < chips - 1)
            def _():
                hid_far_out[order, :, lanes] = total.astype(bf16)

                @pl.when(last_sub)
                def _():
                    hid_far(order).start()

            @pl.when(order == chips - 1)
            def _():
                hid_sum[:, lanes] = total

    def rows_of(part):
        return pl.ds(pl.multiple_of(part * rows2, rows2), rows2)

    def sum_into_block(part, chunk, with_end):
        where = columns_of(chunk)
        block[...] = jnp.dot(
            features[rows_of(part), 0:tokens], grad[:, grad_columns(side, chunk)], preferred_element_type=f32
        ) + jnp.dot(
            features[rows_of(part), tokens : 2 * tokens], pair_grad[0:tokens, where], preferred_element_type=f32
        )

        def add_end():
            block[...] += jnp.dot(
                features[rows_of(part), 2 * tokens : 4 * tokens],
                pair_grad[tokens : 3 * tokens, where],
                preferred_element_type=f32,
            )

        if with_end is True:
            add_end()
        elif with_end is not False:
            pl.when(with_end)(add_end)

    def base_slot(where):
        return jnp.where(jnp.logical_and(where >= 1, where <= line - 3), where + 1, 0)

    def line_copy(chunk, part, slot, target):
        return remote(
            outgoing.at[lax.rem(chunk, plan.window), part],
            incoming.at[slot, :, columns_of(chunk)],
            line_send.at[part, chunk], line_recv.at[slot, chunk], dp=target,
        )

    def send_sum(chunk, part, target, slot, source):
        @pl.when(chunk >= plan.window)
        def _():
            line_copy(chunk - plan.window, part, slot, target).wait_send()

        spot = lax.rem(chunk, plan.window)
        if source is None:
            outgoing[spot, part] = block[...].astype(bf16)
        else:
            has_source, source_slot = source

            @pl.when(has_source)
            def _():
                line_copy(chunk, part, source_slot, target).wait_recv()
                outgoing[spot, part] = (
                    block[...] + incoming[source_slot, :, columns_of(chunk)].astype(f32)
                ).astype(bf16)

            @pl.when(jnp.logical_not(has_source))
            def _():
                outgoing[spot, part] = block[...].astype(bf16)

        line_copy(chunk, part, slot, target).start()

    def up_slot(part):
        return base_slot(place + 1) + part - place - 1

    from_below = jnp.logical_and(place >= 2, jnp.logical_not(is_low))
    from_above = place <= line - 3

    def last_copy(chunk):
        return remote(
            pair_out.at[:, columns_of(chunk)], pair_in.at[:, columns_of(chunk)],
            last_send.at[chunk], last_recv.at[chunk], dp=partner,
        )

    def add_incoming(chunk, slot):
        line_copy(chunk, 0, slot, me).wait_recv()
        block[...] += incoming[slot, :, columns_of(chunk)].astype(f32)

    def settle(chunk):
        student[0:rows, grad_columns(side, chunk)] = block[
            pl.ds(pl.multiple_of(side * rows, rows), rows), :
        ]
        pair_out[:, columns_of(chunk)] = block[
            pl.ds(pl.multiple_of((PAIR - 1 - side) * rows, rows), rows), :
        ].astype(bf16)
        last_copy(chunk).start()

    def result_copy(which, chunk):
        spot = grad_columns(jnp.where(which == 0, side, PAIR - 1 - side), chunk)
        return pltpu.make_async_copy(student.at[0:rows, spot], out_ref.at[:, spot], out_sem.at[which, chunk])

    def early_sums(chunk):
        @pl.loop(0, line - 2)
        def _(index):
            part = jnp.where(next_low, line - 1 - index, index)
            sum_into_block(part, chunk, True)
            send_sum(
                chunk, part, jnp.where(next_low, up, down), jnp.where(next_low, up_slot(part), part), None
            )

    def late_sums(chunk):
        @pl.when(place >= 2)
        def _():
            @pl.loop(0, line - 1 - place)
            def _(index):
                part = line - 1 - index
                sum_into_block(part, chunk, False)
                send_sum(chunk, part, up, up_slot(part), (from_below, base_slot(place) + part - place))

        @pl.when(place <= line - 3)
        def _():
            @pl.loop(0, place)
            def _(part):
                sum_into_block(part, chunk, False)
                send_sum(chunk, part, down, part, (from_above, part))

        sum_into_block(place, chunk, is_next)

        @pl.when(from_below)
        def _():
            add_incoming(chunk, base_slot(place))

        @pl.when(from_above)
        def _():
            add_incoming(chunk, place)

        settle(chunk)

    @pl.loop(0, chunks + plan.last_lag)
    def _(step):
        @pl.when(step < plan.hid_blocks)
        def _():
            hid_block(step)

        @pl.when(step < chunks)
        def _():
            for part in range(plan.halves):
                y_copy(part, step).wait_recv()

            @pl.when(is_end)
            def _():
                for part in range(plan.halves):
                    end_pair(part, step).start()

                @pl.when(step + plan.ahead < chunks)
                def _():
                    for part in range(plan.halves):
                        end_own(part, step + plan.ahead).start()

            @pl.when(is_next)
            def _():
                for part in range(plan.halves):
                    end_own(part, step).wait_recv()
                    end_pair(part, step).wait_recv()
                early_sums(step)

        @pl.when(
            jnp.logical_and(
                jnp.logical_not(is_end),
                jnp.logical_and(step >= plan.lag, step < chunks + plan.lag),
            )
        )
        def _():
            late_sums(step - plan.lag)

        @pl.when(
            jnp.logical_and(is_end, jnp.logical_and(step >= plan.end_lag, step < chunks + plan.end_lag))
        )
        def _():
            chunk = step - plan.end_lag
            sum_into_block(place, chunk, False)
            add_incoming(chunk, 0)
            settle(chunk)

        @pl.when(step >= plan.last_lag)
        def _():
            chunk = step - plan.last_lag
            last_copy(chunk).wait_recv()
            student[0:rows, grad_columns(PAIR - 1 - side, chunk)] = pair_in[:, columns_of(chunk)].astype(f32)
            result_copy(0, chunk).start()
            result_copy(1, chunk).start()

    @pl.loop(min(chunks + plan.last_lag, plan.hid_blocks), plan.hid_blocks)
    def _(index):
        hid_block(index)

    total = hid_sum[...]
    for index in range(chips - 1):
        hid_far(index).wait_recv()
        total = total + hid_far_in[index].astype(f32)
    hid_ref[...] = total.astype(bf16)

    for part in range(plan.halves):
        for step in range(1, chips):
            gather_far(step, part).wait_send()
            gather_pass(step, part).wait_send()
        gather_copy(0, part, v, other_core).wait_send()
        for step in range(1, vocab):
            stat_copy(step, part, v, lax.rem(v + step, vocab)).wait_send()
    for step in range(chips):
        feature_y(step).wait_send()
        feature_core(1, step).wait_send()
        hid_core(step).wait_send()
    for index in range(chips - 1):
        hid_far(index).wait_send()

    @pl.when(is_end)
    def _():
        for which in range(2):
            feature_z(which).wait_send()

        @pl.loop(0, chunks)
        def _(chunk):
            for part in range(plan.halves):
                end_own(part, chunk).wait_send()
                end_pair(part, chunk).wait_send()

    @pl.when(is_next)
    def _():
        for which in (2, 3):
            feature_core(which, 0).wait_send()
            for step in range(1, chips):
                feature_x(which, step).wait_send()
                feature_core(which, step).wait_send()

    @pl.loop(0, chunks)
    def _(chunk):
        for part in range(plan.halves):
            y_copy(part, chunk).wait_send()
        last_copy(chunk).wait_send()
        result_copy(0, chunk).wait()
        result_copy(1, chunk).wait()

    @pl.when(jnp.logical_not(is_end))
    def _():
        @pl.loop(chunks - plan.window, chunks)
        def _(chunk):
            @pl.loop(0, place)
            def _(part):
                line_copy(chunk, part, 0, down).wait_send()

            @pl.loop(place + 1, line)
            def _(part):
                line_copy(chunk, part, 0, up).wait_send()


def per_device(shards, vocab, hidden_states, teacher_logits, head_weight):
    tokens, shard = hidden_states.shape
    model_width, columns = head_weight.shape
    plan = Plan(shards, vocab, tokens, shard, model_width, columns)
    dma = pltpu.SemaphoreType.DMA
    chips, halves, chunks = plan.chips, plan.halves, plan.chunks
    any_space = pl.BlockSpec(memory_space=pl.ANY)
    in_vmem = pl.BlockSpec(memory_space=pltpu.VMEM)
    divergence, hidden_grad, head_grad = pl.pallas_call(
        functools.partial(fused_kernel, plan),
        out_shape=(
            jax.ShapeDtypeStruct((1, tokens), f32),
            jax.ShapeDtypeStruct((tokens, shard), bf16),
            jax.ShapeDtypeStruct((plan.rows, columns), f32),
        ),
        in_specs=[any_space] * 3,
        out_specs=(in_vmem, in_vmem, any_space),
        scratch_shapes=[
            pltpu.VMEM((model_width, columns), bf16),
            pltpu.VMEM((tokens, columns), f32),
            pltpu.VMEM((tokens, columns), bf16),
            pltpu.VMEM((tokens, model_width), bf16),
            pltpu.VMEM((model_width, 4 * tokens), bf16),
            pltpu.VMEM((3 * tokens, plan.half), bf16),
            pltpu.VMEM((plan.slots, plan.rows2, plan.half), bf16),
            pltpu.VMEM((plan.window, plan.line, plan.rows2, plan.width), bf16),
            pltpu.VMEM((plan.rows2, plan.width), f32),
            pltpu.VMEM((plan.rows, plan.half), bf16),
            pltpu.VMEM((plan.rows, plan.half), bf16),
            pltpu.VMEM((chips, tokens, shard), bf16),
            pltpu.VMEM((chips, tokens, shard), bf16),
            pltpu.VMEM((chips - 1, tokens, shard), bf16),
            pltpu.VMEM((chips - 1, tokens, shard), bf16),
            pltpu.VMEM((tokens, shard), f32),
            pltpu.VMEM((tokens, LANES), f32),
            pltpu.VMEM((tokens, LANES), f32),
            pltpu.VMEM((3, tokens, LANES), f32),
            pltpu.VMEM((vocab, 8, tokens), f32),
            dma((2,)), dma((chips,)), dma((2, chunks)),
            dma((2 * chips - 1, halves)), dma((2 * chips - 1, halves)),
            dma((chips,)), dma((chips,)),
            dma((2,)), dma((2,)),
            dma((2, chips)), dma((2, chips)),
            dma((3, chips)), dma((3, chips)),
            dma((vocab, halves)), dma((vocab, halves)),
            dma((halves, chunks)), dma((halves, chunks)),
            dma((halves, chunks)), dma((halves, chunks)),
            dma((halves, chunks)), dma((halves, chunks)),
            dma((plan.line, chunks)), dma((plan.slots, chunks)),
            dma((chunks,)), dma((chunks,)),
            dma((chips,)), dma((chips,)),
            dma((chips - 1,)), dma((chips - 1,)),
        ],
        compiler_params=pltpu.CompilerParams(
            collective_id=0, has_side_effects=True, vmem_limit_bytes=67043328
        ),
    )(hidden_states, teacher_logits, head_weight)
    return divergence.reshape(tokens), hidden_grad, head_grad


def solution(mesh):
    in_specs = (P("dp", "vocab"), P("dp", "vocab"), P(None, "vocab"))
    out_specs = (P("dp"), P("dp", "vocab"), P("dp", "vocab"))
    return jax.shard_map(
        functools.partial(per_device, mesh.shape["dp"], mesh.shape["vocab"]),
        mesh=mesh, in_specs=in_specs, out_specs=out_specs, check_vma=False,
    )
```

time: 300 us -> 189 us (0.63)
  waiting for transfers between devices: 31.1 us -> 0 us
  matrix products: 25.4 us -> 0 us
  Pallas kernels: 197 us -> 180 us
  other arithmetic: 14.6 us -> 0 us
  between operations: 14.2 us -> 0.64 us
  blocking collectives: 5.22 us -> 0 us
    dot_general x2 -> x0, matrix products: 25.4 us -> none  [the longest x1 13.4 us: per_device(): lax.dot_general(logit_grad, head_weight, (((1,), (1,)), ((), ())), prefer...]
    all_gather x1 -> x0, waiting for transfers between devices: 23.2 us -> none  [per_device(): gathered = lax.all_gather(hidden_states, 'vocab', axis=1, tiled=True)]
    pallas_call x1, Pallas kernels: 197 us -> 180 us  [per_device(): pl.pallas_call(functools.partial(fused_kernel, plan), out_shape=(jax.Shap...]
    ppermute x1 -> x0, waiting for transfers between devices: 7.83 us -> none  [per_device(): received = lax.ppermute(given, 'dp', swap)]
    convert_element_type x1 -> x0, other arithmetic: 5.36 us -> none  [per_device(): logit_grad = (grad_scale * (jnp.exp(student - student_log[:, None]) - jnp...]
    all_gather x1 -> x0, blocking collectives: 5.22 us -> none  [per_device(): stats = lax.all_gather(stats, 'vocab', axis=0, tiled=False)]
    reduce_sum x2 -> x0, other arithmetic: 3.94 us -> none  [the longest x1 3.9 us: per_device(): jnp.sum(teacher_terms * (teacher - student), axis=1)]
    unnamed x12 -> x3, local copies, waits for them, and re-layouts: 8.73 us -> 7.77 us
  transfers between devices with their start and end apart: 3 -> 0, of which waited for: 2 -> 0; matrix products, arithmetic and copies ran while one was open for 6% -> 0% of each run, Pallas kernels for 66% -> 0%
where the time goes in v1:
time: 189 us
  Pallas kernels  180 us (95%)
  local copies, waits for them, and re-layouts  7.77 us (4%)
    pallas_call x1, Pallas kernels, per_device(): pl.pallas_call(functools.partial(fused_kernel, plan), out_shape=(jax.Shap...  180 us
    unnamed x3, local copies, waits for them, and re-layouts  7.77 us

profile of v1, /device:TPU:0, one launch (start us, length us, event | category | flops | bytes accessed | tf_op | source)
XLA Modules:
  0.0 188.9 jit_solution(6075498005270568366)
XLA Ops:
  0.6 180.5 %shard_map.58 = (f32[1,512]{1,0:T(1,128)}, bf16[512,512]{1,0:T(8,128)(2,1)}, f32[256,4096]{1,0:T(8,128)}) custom-call(bf16[512,512]{1,0:T(8,128)(2,1)} %hidden_ref.1, bf16[512,4096]{1,0:T(8,128)(2,1)} %teacher_ref.1, bf16[2048,4096]{1,0:T(8,128)(2,1)} %weight_ref.1), custom_call_target="tpu_custom_call" | custom-call | tf_op jit(solution)/shard_map/pallas_call | solution.py:687
  181.1 1.2 copy.9
  182.3 1.9 copy.10
  184.2 4.7 %copy.11 = f32[256,4096]{1,0:T(8,128)} copy(f32[256,4096]{1,0:T(8,128)} %get-tuple-element.14) | data formatting | bytes 8388608

commit v2 on v1

--- a/solution.py
+++ b/solution.py
@@ -1,4 +1,5 @@
 import functools
+import math
 
 import jax
 import jax.numpy as jnp
@@ -33,10 +34,12 @@
         self.rows2 = model_width // self.line
         self.rows = self.rows2 // PAIR
         self.window = min(3, self.chunks)
+        self.dot_width = min(512, columns)
         self.lag = min(2, self.chunks)
         self.end_lag = self.lag + 2
         self.last_lag = self.end_lag + 1
         self.ahead = min(2, self.chunks)
+        self.first = min(2, self.chunks)
         self.hid_width = min(256, shard)
         self.hid_subs = shard // self.hid_width
         self.hid_blocks = vocab * self.hid_subs
@@ -110,9 +113,20 @@
     own_load = pltpu.make_async_copy(hidden_ref, gathered.at[:, shard_of(v)], load_sem.at[0])
     teacher_load = pltpu.make_async_copy(teacher_ref, grad, load_sem.at[1])
 
-    def weight_load(step):
-        part = chip_rows(chip_before(step))
-        return pltpu.make_async_copy(weight_ref.at[part, :], weight.at[part, :], weight_sem.at[step])
+    dot_width = plan.dot_width
+    dot_blocks = columns // dot_width
+
+    def dot_columns(index):
+        return pl.ds(pl.multiple_of(index * dot_width, dot_width), dot_width)
+
+    def weight_load(step, index):
+        spot = (chip_rows(chip_before(step)), dot_columns(index))
+        return pltpu.make_async_copy(weight_ref.at[spot], weight.at[spot], weight_sem.at[step, index])
+
+    def load_weights(step):
+        @pl.loop(0, dot_blocks)
+        def _(index):
+            weight_load(step, index).start()
 
     barrier = pltpu.get_barrier_semaphore()
     for step in range(1, vocab):
@@ -130,10 +144,10 @@
         pl.semaphore_signal(barrier, inc=1, device_id={"dp": up}, device_id_type=MESH)
 
     own_load.start()
-    weight_load(0).start()
+    load_weights(0)
     teacher_load.start()
     for step in range(1, chips):
-        weight_load(step).start()
+        load_weights(step)
     own_load.wait()
     pl.semaphore_wait(barrier, vocab + has_down.astype(jnp.int32) + has_up.astype(jnp.int32))
 
@@ -152,99 +166,112 @@
             gather_far(step, part).start()
         gather_copy(0, part, v, other_core).start()
 
-    def set_ref(which, index):
-        return features.at[shard_of(index), pl.ds(which * tokens, tokens)]
-
-    def turn(index):
-        features[shard_of(index), 0:tokens] = gathered[:, shard_of(index)].T
-
-    def feature_y(step):
+    def set_ref(which, index, part):
+        return features.at[shard_of(index), pl.ds(which * tokens + part * half_tokens, half_tokens)]
+
+    def turn(index, part):
+        features[shard_of(index), part * half_tokens : (part + 1) * half_tokens] = gathered[
+            token_half(part), shard_of(index)
+        ].T
+
+    def feature_y(step, part):
         index = chip_before(step) * CORES + core
-        return remote(set_ref(0, index), set_ref(1, index), fy_send.at[step], fy_recv.at[step], dp=partner)
-
-    def feature_z(which):
-        return remote(set_ref(which, v), set_ref(2 + which, v), fz_send.at[which], fz_recv.at[which], dp=inner)
-
-    def feature_x(which, step):
-        ref = set_ref(which, v)
-        return remote(
-            ref, ref, fx_send.at[which - 2, step], fx_recv.at[which - 2, step],
+        return remote(
+            set_ref(0, index, part), set_ref(1, index, part), fy_send.at[step, part], fy_recv.at[step, part],
+            dp=partner,
+        )
+
+    def feature_z(which, part):
+        return remote(
+            set_ref(which, v, part), set_ref(2 + which, v, part), fz_send.at[which, part], fz_recv.at[which, part],
+            dp=inner,
+        )
+
+    def feature_x(which, step, part):
+        ref = set_ref(which, v, part)
+        return remote(
+            ref, ref, fx_send.at[which - 2, step, part], fx_recv.at[which - 2, step, part],
             vocab=chip_after(step) * CORES + core,
         )
 
-    def feature_core(which, step):
-        ref = set_ref(which, chip_before(step) * CORES + core)
-        return remote(ref, ref, fc_send.at[which - 1, step], fc_recv.at[which - 1, step], vocab=other_core)
-
-    turn(v)
-    feature_y(0).start()
-
-    @pl.when(is_end)
-    def _():
-        feature_z(0).start()
+    def feature_core(which, step, part):
+        ref = set_ref(which, chip_before(step) * CORES + core, part)
+        return remote(
+            ref, ref, fc_send.at[which - 1, step, part], fc_recv.at[which - 1, step, part], vocab=other_core
+        )
+
+    for part in range(plan.halves):
+        turn(v, part)
+        feature_y(0, part).start()
+
+        @pl.when(is_end)
+        def _():
+            feature_z(0, part).start()
 
     for part in range(plan.halves):
         gather_copy(0, part, other_core, other_core).wait_recv()
-    weight_load(0).wait()
-    dot_width = min(512, columns)
-
-    @pl.loop(0, columns // dot_width)
-    def _(index):
-        where = pl.ds(pl.multiple_of(index * dot_width, dot_width), dot_width)
-        student[:, where] = jnp.dot(
-            gathered[:, chip_rows(chip)], weight[chip_rows(chip), where], preferred_element_type=f32
-        )
-
+
+    def local_logits():
+        @pl.loop(0, dot_blocks)
+        def _(index):
+            where = dot_columns(index)
+            weight_load(0, index).wait()
+            student[:, where] = jnp.dot(
+                gathered[:, chip_rows(chip)], weight[chip_rows(chip), where], preferred_element_type=f32
+            )
+
+    band = 32
+
+    def teacher_tops():
+        @pl.loop(0, tokens // band)
+        def _(index):
+            where = pl.ds(pl.multiple_of(index * band, band), band)
+            top = grad[where, 0:LANES]
+            for column in range(1, columns // LANES):
+                top = jnp.maximum(top, grad[where, column * LANES : (column + 1) * LANES])
+            lane_stats[0, where, :] = top.astype(f32)
+
+        row_teacher[...] = jnp.broadcast_to(jnp.max(lane_stats[0], axis=1, keepdims=True), (tokens, LANES))
+
+    local_logits()
     teacher_load.wait()
-    band = 32
-
-    @pl.loop(0, tokens // band)
-    def _(index):
-        where = pl.ds(pl.multiple_of(index * band, band), band)
-        top = grad[where, 0:LANES]
-        for column in range(1, columns // LANES):
-            top = jnp.maximum(top, grad[where, column * LANES : (column + 1) * LANES])
-        lane_stats[0, where, :] = top.astype(f32)
-
-    row_teacher[...] = jnp.broadcast_to(jnp.max(lane_stats[0], axis=1, keepdims=True), (tokens, LANES))
-    turn(other_core)
+    teacher_tops()
+    for part in range(plan.halves):
+        turn(other_core, part)
 
     def stat_copy(step, part, owner, target):
         ref = stats.at[owner, :, token_half(part)]
         return remote(ref, ref, stat_send.at[step, part], stat_recv.at[step, part], vocab=target)
 
-    def first_half(part):
-        where_rows = token_half(part)
-        for step in range(1, chips):
-            gather_copy(step, part, chip_before(step) * CORES + core, other_core).wait_recv()
-            gather_pass(step, part).start()
+    def await_far(part):
         for step in range(1, chips):
             gather_copy(
                 chips - 1 + step, part, chip_before(step) * CORES + (CORES - 1) - core, other_core
             ).wait_recv()
-        if part == 0:
-            for step in range(1, chips):
-                weight_load(step).wait()
-        lane_stats[0, where_rows, :] = jnp.full((half_tokens, LANES), -jnp.inf, f32)
-
-        @pl.loop(0, columns // dot_width)
+
+    def far_logits():
+        lane_stats[0] = jnp.full((tokens, LANES), -jnp.inf, f32)
+
+        @pl.loop(0, dot_blocks)
         def _(index):
-            where = pl.ds(pl.multiple_of(index * dot_width, dot_width), dot_width)
-            total = student[where_rows, where]
+            where = dot_columns(index)
+            total = student[:, where]
             for step in range(1, chips):
                 far = chip_rows(chip_before(step))
-                total = total + jnp.dot(
-                    gathered[where_rows, far], weight[far, where], preferred_element_type=f32
-                )
-            student[where_rows, where] = total
-            top = lane_stats[0, where_rows, :]
+                weight_load(step, index).wait()
+                total = total + jnp.dot(gathered[:, far], weight[far, where], preferred_element_type=f32)
+            student[:, where] = total
+            top = lane_stats[0]
             for column in range(dot_width // LANES):
                 top = jnp.maximum(top, total[:, column * LANES : (column + 1) * LANES])
-            lane_stats[0, where_rows, :] = top
-
+            lane_stats[0] = top
+
+    def student_tops(part):
+        where_rows = token_half(part)
         student_top = jnp.max(lane_stats[0, where_rows, :], axis=1, keepdims=True)
         row_student[where_rows, :] = jnp.broadcast_to(student_top, (half_tokens, LANES))
 
+    def row_sums(part):
         @pl.loop(0, half_tokens // band)
         def _(index):
             where = pl.ds(pl.multiple_of(part * half_tokens + index * band, band), band)
@@ -254,12 +281,16 @@
                 lanes = slice(column * LANES, (column + 1) * LANES)
                 logit, target = student[where, lanes], grad[where, lanes].astype(f32)
                 term = jnp.exp(target - teacher_max)
-                sums[0] += jnp.exp(logit - student_max)
+                student_term = jnp.exp(logit - student_max)
+                student[where, lanes] = student_term
+                sums[0] += student_term
                 sums[1] += term
                 sums[2] += term * (target - logit)
             for which in range(3):
                 lane_stats[which, where, :] = sums[which]
 
+    def send_stats(part):
+        where_rows = token_half(part)
         lane = lax.broadcasted_iota(jnp.int32, (half_tokens, LANES), 1)
         packed = jnp.where(lane == 0, row_student[where_rows, :], row_teacher[where_rows, :])
         for which in range(3):
@@ -269,6 +300,11 @@
         for step in range(1, vocab):
             stat_copy(step, part, v, lax.rem(v + step, vocab)).start()
 
+    def pass_on(part):
+        for step in range(1, chips):
+            gather_copy(step, part, chip_before(step) * CORES + core, other_core).wait_recv()
+            gather_pass(step, part).start()
+
     def y_copy(part, chunk):
         return remote(
             grad.at[token_half(part), grad_columns(PAIR - 1 - side, chunk)],
@@ -290,7 +326,7 @@
             zf_send.at[part, chunk], zf_recv.at[part, chunk], dp=inner,
         )
 
-    def second_half(part):
+    def combine(part):
         where_rows = token_half(part)
         for step in range(1, vocab):
             stat_copy(step, part, lax.rem(v + vocab - step, vocab), other_core).wait_recv()
@@ -304,27 +340,30 @@
         student_log = student_max + jnp.log(student_total)
         teacher_log = teacher_max + jnp.log(teacher_total)
         kl_ref[:, where_rows] = cross / teacher_total - teacher_log + student_log
+        student_scale = grad_scale * jnp.exp(stats[v, 0:1, where_rows] - student_log)
         row = lax.broadcasted_iota(jnp.int32, (LANES, half_tokens), 0)
         packed = jnp.where(
             row == 0,
-            jnp.broadcast_to(student_log, (LANES, half_tokens)),
-            jnp.broadcast_to(teacher_log, (LANES, half_tokens)),
+            jnp.broadcast_to(student_scale, (LANES, half_tokens)),
+            jnp.broadcast_to(teacher_log - math.log(grad_scale), (LANES, half_tokens)),
         ).T
         row_student[where_rows, :] = jnp.broadcast_to(packed[:, 0:1], (half_tokens, LANES))
         row_teacher[where_rows, :] = jnp.broadcast_to(packed[:, 1:2], (half_tokens, LANES))
 
+    def grads(part):
         @pl.loop(0, half_tokens // band)
         def _(index):
             where = pl.ds(pl.multiple_of(part * half_tokens + index * band, band), band)
             student_row, teacher_row = row_student[where, :], row_teacher[where, :]
             for column in range(columns // LANES):
                 lanes = slice(column * LANES, (column + 1) * LANES)
-                value = jnp.exp(student[where, lanes] - student_row) - jnp.exp(
+                value = student[where, lanes] * student_row - jnp.exp(
                     grad[where, lanes].astype(f32) - teacher_row
                 )
-                grad[where, lanes] = (grad_scale * value).astype(bf16)
-
-        @pl.loop(0, chunks)
+                grad[where, lanes] = value.astype(bf16)
+
+    def send_grads(part):
+        @pl.loop(0, plan.first)
         def _(chunk):
             y_copy(part, chunk).start()
 
@@ -333,55 +372,88 @@
             for chunk in range(plan.ahead):
                 end_own(part, chunk).start()
 
-    def first_service():
-        feature_y(0).wait_recv()
-        feature_core(1, 0).start()
+        if part == plan.halves - 1:
+
+            @pl.loop(plan.first, chunks)
+            def _(chunk):
+                for each in range(plan.halves):
+                    y_copy(each, chunk).start()
+
+    def first_service(part):
+        feature_y(0, part).wait_recv()
+        feature_core(1, 0, part).start()
 
         @pl.when(is_end)
         def _():
-            feature_z(1).start()
+            feature_z(1, part).start()
 
         @pl.when(is_next)
         def _():
-            feature_z(0).wait_recv()
+            feature_z(0, part).wait_recv()
             for step in range(1, chips):
-                feature_x(2, step).start()
-            feature_core(2, 0).start()
-
+                feature_x(2, step, part).start()
+            feature_core(2, 0, part).start()
+
+    def turn_far(part):
         for step in range(1, chips):
-            turn(chip_before(step) * CORES + core)
-            feature_y(step).start()
+            turn(chip_before(step) * CORES + core, part)
+            feature_y(step, part).start()
         for step in range(1, chips):
-            turn(chip_before(step) * CORES + (CORES - 1) - core)
-
-    def second_service():
+            turn(chip_before(step) * CORES + (CORES - 1) - core, part)
+
+    def middle_service(part):
+        @pl.when(is_next)
+        def _():
+            feature_z(1, part).wait_recv()
+            for step in range(1, chips):
+                feature_x(3, step, part).start()
+            feature_core(3, 0, part).start()
+            for step in range(1, chips):
+                feature_x(2, step, part).wait_recv()
+                feature_core(2, step, part).start()
+
+    def second_service(part):
         for step in range(1, chips):
-            feature_y(step).wait_recv()
-            feature_core(1, step).start()
-
+            feature_y(step, part).wait_recv()
+            feature_core(1, step, part).start()
+
+    def last_service(part):
         @pl.when(is_next)
         def _():
-            feature_z(1).wait_recv()
             for step in range(1, chips):
-                feature_x(3, step).start()
-            feature_core(3, 0).start()
-            for which in (2, 3):
-                for step in range(1, chips):
-                    feature_x(which, step).wait_recv()
-                    feature_core(which, step).start()
+                feature_x(3, step, part).wait_recv()
+                feature_core(3, step, part).start()
+
+    def await_features(part):
+        for step in range(chips):
+            feature_core(1, step, part).wait_recv()
+
+        @pl.when(is_next)
+        def _():
             for which in (2, 3):
                 for step in range(chips):
-                    feature_core(which, step).wait_recv()
-
-        for step in range(chips):
-            feature_core(1, step).wait_recv()
-
-    first_half(0)
-    first_half(1)
-    second_half(0)
-    first_service()
-    second_half(1)
-    second_service()
+                    feature_core(which, step, part).wait_recv()
+
+    every = range(plan.halves)
+    for part in every:
+        pass_on(part)
+        first_service(part)
+        await_far(part)
+        turn_far(part)
+    far_logits()
+    for part in every:
+        student_tops(part)
+        row_sums(part)
+        send_stats(part)
+    for part in every:
+        middle_service(part)
+    for part in every:
+        combine(part)
+        grads(part)
+        send_grads(part)
+    for service in (second_service, last_service, await_features):
+        for part in every:
+            service(part)
 
     def hid_core(index):
         return remote(
@@ -435,6 +507,17 @@
             def _():
                 hid_sum[:, lanes] = total
 
+    def hid_finish():
+        total = hid_sum[...]
+        for index in range(chips - 1):
+            hid_far(index).wait_recv()
+            total = total + hid_far_in[index].astype(f32)
+        hid_ref[...] = total.astype(bf16)
+        for step in range(chips):
+            hid_core(step).wait_send()
+        for index in range(chips - 1):
+            hid_far(index).wait_send()
+
     def rows_of(part):
         return pl.ds(pl.multiple_of(part * rows2, rows2), rows2)
 
@@ -558,11 +641,54 @@
 
         settle(chunk)
 
+    def drain():
+        for part in every:
+            for step in range(1, chips):
+                gather_far(step, part).wait_send()
+                gather_pass(step, part).wait_send()
+            gather_copy(0, part, v, other_core).wait_send()
+            for step in range(1, vocab):
+                stat_copy(step, part, v, lax.rem(v + step, vocab)).wait_send()
+            for step in range(chips):
+                feature_y(step, part).wait_send()
+                feature_core(1, step, part).wait_send()
+
+            @pl.when(is_end)
+            def _():
+                for which in range(2):
+                    feature_z(which, part).wait_send()
+
+            @pl.when(is_next)
+            def _():
+                for which in (2, 3):
+                    feature_core(which, 0, part).wait_send()
+                    for step in range(1, chips):
+                        feature_x(which, step, part).wait_send()
+                        feature_core(which, step, part).wait_send()
+
+        @pl.loop(0, chunks)
+        def _(chunk):
+            for part in every:
+                y_copy(part, chunk).wait_send()
+
+        @pl.when(is_end)
+        def _():
+            @pl.loop(0, chunks)
+            def _(chunk):
+                for part in every:
+                    end_own(part, chunk).wait_send()
+                    end_pair(part, chunk).wait_send()
+
     @pl.loop(0, chunks + plan.last_lag)
     def _(step):
         @pl.when(step < plan.hid_blocks)
         def _():
             hid_block(step)
+
+        if plan.hid_blocks < chunks + plan.last_lag:
+            pl.when(step == max(plan.hid_blocks, chunks))(hid_finish)
+
+        pl.when(step == chunks + plan.lag - 1)(drain)
 
         @pl.when(step < chunks)
         def _():
@@ -616,49 +742,11 @@
     def _(index):
         hid_block(index)
 
-    total = hid_sum[...]
-    for index in range(chips - 1):
-        hid_far(index).wait_recv()
-        total = total + hid_far_in[index].astype(f32)
-    hid_ref[...] = total.astype(bf16)
-
-    for part in range(plan.halves):
-        for step in range(1, chips):
-            gather_far(step, part).wait_send()
-            gather_pass(step, part).wait_send()
-        gather_copy(0, part, v, other_core).wait_send()
-        for step in range(1, vocab):
-            stat_copy(step, part, v, lax.rem(v + step, vocab)).wait_send()
-    for step in range(chips):
-        feature_y(step).wait_send()
-        feature_core(1, step).wait_send()
-        hid_core(step).wait_send()
-    for index in range(chips - 1):
-        hid_far(index).wait_send()
-
-    @pl.when(is_end)
-    def _():
-        for which in range(2):
-            feature_z(which).wait_send()
-
-        @pl.loop(0, chunks)
-        def _(chunk):
-            for part in range(plan.halves):
-                end_own(part, chunk).wait_send()
-                end_pair(part, chunk).wait_send()
-
-    @pl.when(is_next)
-    def _():
-        for which in (2, 3):
-            feature_core(which, 0).wait_send()
-            for step in range(1, chips):
-                feature_x(which, step).wait_send()
-                feature_core(which, step).wait_send()
+    if plan.hid_blocks >= chunks + plan.last_lag:
+        hid_finish()
 
     @pl.loop(0, chunks)
     def _(chunk):
-        for part in range(plan.halves):
-            y_copy(part, chunk).wait_send()
         last_copy(chunk).wait_send()
         result_copy(0, chunk).wait()
         result_copy(1, chunk).wait()
@@ -714,12 +802,12 @@
             pltpu.VMEM((tokens, LANES), f32),
             pltpu.VMEM((3, tokens, LANES), f32),
             pltpu.VMEM((vocab, 8, tokens), f32),
-            dma((2,)), dma((chips,)), dma((2, chunks)),
+            dma((2,)), dma((chips, columns // plan.dot_width)), dma((2, chunks)),
             dma((2 * chips - 1, halves)), dma((2 * chips - 1, halves)),
-            dma((chips,)), dma((chips,)),
-            dma((2,)), dma((2,)),
-            dma((2, chips)), dma((2, chips)),
-            dma((3, chips)), dma((3, chips)),
+            dma((chips, halves)), dma((chips, halves)),
+            dma((2, halves)), dma((2, halves)),
+            dma((2, chips, halves)), dma((2, chips, halves)),
+            dma((3, chips, halves)), dma((3, chips, halves)),
             dma((vocab, halves)), dma((vocab, halves)),
             dma((halves, chunks)), dma((halves, chunks)),
             dma((halves, chunks)), dma((halves, chunks)),

time: 189 us -> 161 us (0.85)
  Pallas kernels: 180 us -> 152 us
    pallas_call x1, Pallas kernels: 180 us -> 152 us  [per_device(): pl.pallas_call(functools.partial(fused_kernel, plan), out_shape=(jax.Shap...]
where the time goes in v2:
time: 161 us
  Pallas kernels  152 us (94%)
  local copies, waits for them, and re-layouts  7.77 us (5%)
    pallas_call x1, Pallas kernels, per_device(): pl.pallas_call(functools.partial(fused_kernel, plan), out_shape=(jax.Shap...  152 us
    unnamed x3, local copies, waits for them, and re-layouts  7.77 us

profile of v2, /device:TPU:0, one launch (start us, length us, event | category | flops | bytes accessed | tf_op | source)
XLA Modules:
  0.0 160.8 jit_solution(10359284371012186381)
XLA Ops:
  0.6 152.4 %shard_map.58 = (f32[1,512]{1,0:T(1,128)}, bf16[512,512]{1,0:T(8,128)(2,1)}, f32[256,4096]{1,0:T(8,128)}) custom-call(bf16[512,512]{1,0:T(8,128)(2,1)} %hidden_ref.1, bf16[512,4096]{1,0:T(8,128)(2,1)} %teacher_ref.1, bf16[2048,4096]{1,0:T(8,128)(2,1)} %weight_ref.1), custom_call_target="tpu_custom_call" | custom-call | tf_op jit(solution)/shard_map/pallas_call | solution.py:775
  153.1 1.2 copy.9
  154.3 1.9 %copy.10 = bf16[512,512]{1,0:T(8,128)(2,1)} copy(bf16[512,512]{1,0:T(8,128)(2,1)} %get-tuple-element.13) | data formatting | bytes 1048576
  156.2 4.7 %copy.11 = f32[256,4096]{1,0:T(8,128)} copy(f32[256,4096]{1,0:T(8,128)} %get-tuple-element.14) | data formatting | bytes 8388608

commit v3 on v2

--- a/solution.py
+++ b/solution.py
@@ -28,18 +28,19 @@
         self.columns = columns
         self.halves = 2
         self.half_tokens = tokens // self.halves
+        self.half_shard = shard // self.halves
         self.half = columns // PAIR
-        self.width = min(256, self.half)
+        self.width = min(128, self.half)
         self.chunks = self.half // self.width
         self.rows2 = model_width // self.line
         self.rows = self.rows2 // PAIR
-        self.window = min(3, self.chunks)
+        self.window = min(6, self.chunks)
         self.dot_width = min(512, columns)
-        self.lag = min(2, self.chunks)
+        self.lag = 2
         self.end_lag = self.lag + 2
-        self.last_lag = self.end_lag + 1
-        self.ahead = min(2, self.chunks)
-        self.first = min(2, self.chunks)
+        self.last_lag = max(self.end_lag + 1, self.chunks // 2 + 2)
+        self.ahead = 2
+        self.first = 2
         self.hid_width = min(256, shard)
         self.hid_subs = shard // self.hid_width
         self.hid_blocks = vocab * self.hid_subs
@@ -49,12 +50,12 @@
 def fused_kernel(
     plan,
     hidden_ref, teacher_ref, weight_ref,
-    kl_ref, hid_ref, out_ref,
-    weight, student, grad, gathered, features, pair_grad, incoming, outgoing, block,
+    kl_any, hid_any, own_any, pair_any,
+    kl_ref, hid_ref, weight, student, grad, gathered, features, pair_grad, incoming, outgoing, block,
     pair_out, pair_in, hid_out, hid_in, hid_far_out, hid_far_in, hid_sum,
     row_student, row_teacher, lane_stats, stats,
     load_sem, weight_sem, out_sem,
-    gather_send, gather_recv, fy_send, fy_recv, fz_send, fz_recv, fx_send, fx_recv, fc_send, fc_recv,
+    gather_send, gather_recv, fy_send, fy_recv, fz_send, fz_recv, fzf_send, fzf_recv, fx_send, fx_recv, fc_send, fc_recv,
     stat_send, stat_recv, y_send, y_recv, zo_send, zo_recv, zf_send, zf_recv,
     line_send, line_recv, last_send, last_recv,
     hc_send, hc_recv, hx_send, hx_recv,
@@ -151,8 +152,13 @@
     own_load.wait()
     pl.semaphore_wait(barrier, vocab + has_down.astype(jnp.int32) + has_up.astype(jnp.int32))
 
+    half_shard = plan.half_shard
+
+    def shard_half(index, part):
+        return pl.ds(pl.multiple_of(index * shard + part * half_shard, half_shard), half_shard)
+
     def gather_copy(index, part, column, target):
-        ref = gathered.at[token_half(part), shard_of(column)]
+        ref = gathered.at[:, shard_half(column, part)]
         return remote(ref, ref, gather_send.at[index, part], gather_recv.at[index, part], vocab=target)
 
     def gather_far(step, part):
@@ -167,12 +173,10 @@
         gather_copy(0, part, v, other_core).start()
 
     def set_ref(which, index, part):
-        return features.at[shard_of(index), pl.ds(which * tokens + part * half_tokens, half_tokens)]
+        return features.at[shard_half(index, part), pl.ds(which * tokens, tokens)]
 
     def turn(index, part):
-        features[shard_of(index), part * half_tokens : (part + 1) * half_tokens] = gathered[
-            token_half(part), shard_of(index)
-        ].T
+        features[shard_half(index, part), 0:tokens] = gathered[:, shard_half(index, part)].T
 
     def feature_y(step, part):
         index = chip_before(step) * CORES + core
@@ -186,6 +190,10 @@
             set_ref(which, v, part), set_ref(2 + which, v, part), fz_send.at[which, part], fz_recv.at[which, part],
             dp=inner,
         )
+
+    def feature_z_far(step):
+        index = chip_before(step) * CORES + core
+        return remote(set_ref(1, index, 0), set_ref(3, index, 0), fzf_send.at[step], fzf_recv.at[step], dp=inner)
 
     def feature_x(which, step, part):
         ref = set_ref(which, v, part)
@@ -249,22 +257,30 @@
                 chips - 1 + step, part, chip_before(step) * CORES + (CORES - 1) - core, other_core
             ).wait_recv()
 
-    def far_logits():
-        lane_stats[0] = jnp.full((tokens, LANES), -jnp.inf, f32)
+    def far_logits(part):
+        last = part == plan.halves - 1
+        if last:
+            lane_stats[0] = jnp.full((tokens, LANES), -jnp.inf, f32)
 
         @pl.loop(0, dot_blocks)
         def _(index):
             where = dot_columns(index)
             total = student[:, where]
             for step in range(1, chips):
-                far = chip_rows(chip_before(step))
-                weight_load(step, index).wait()
-                total = total + jnp.dot(gathered[:, far], weight[far, where], preferred_element_type=f32)
+                far = [chip_before(step) * CORES + each for each in range(CORES)]
+                if part == 0:
+                    weight_load(step, index).wait()
+                total = total + jnp.dot(
+                    jnp.concatenate([gathered[:, shard_half(each, part)] for each in far], axis=1),
+                    jnp.concatenate([weight[shard_half(each, part), where] for each in far], axis=0),
+                    preferred_element_type=f32,
+                )
             student[:, where] = total
-            top = lane_stats[0]
-            for column in range(dot_width // LANES):
-                top = jnp.maximum(top, total[:, column * LANES : (column + 1) * LANES])
-            lane_stats[0] = top
+            if last:
+                top = lane_stats[0]
+                for column in range(dot_width // LANES):
+                    top = jnp.maximum(top, total[:, column * LANES : (column + 1) * LANES])
+                lane_stats[0] = top
 
     def student_tops(part):
         where_rows = token_half(part)
@@ -405,8 +421,9 @@
         @pl.when(is_next)
         def _():
             feature_z(1, part).wait_recv()
-            for step in range(1, chips):
-                feature_x(3, step, part).start()
+            if part > 0:
+                for step in range(1, chips):
+                    feature_x(3, step, part).start()
             feature_core(3, 0, part).start()
             for step in range(1, chips):
                 feature_x(2, step, part).wait_recv()
@@ -417,11 +434,17 @@
             feature_y(step, part).wait_recv()
             feature_core(1, step, part).start()
 
+            if part == 0:
+                pl.when(is_end)(feature_z_far(step).start)
+
     def last_service(part):
         @pl.when(is_next)
         def _():
             for step in range(1, chips):
-                feature_x(3, step, part).wait_recv()
+                if part > 0:
+                    feature_x(3, step, part).wait_recv()
+                else:
+                    feature_z_far(step).wait_recv()
                 feature_core(3, step, part).start()
 
     def await_features(part):
@@ -440,7 +463,8 @@
         first_service(part)
         await_far(part)
         turn_far(part)
-    far_logits()
+        far_logits(part)
+    second_service(0)
     for part in every:
         student_tops(part)
         row_sums(part)
@@ -451,9 +475,12 @@
         combine(part)
         grads(part)
         send_grads(part)
-    for service in (second_service, last_service, await_features):
-        for part in every:
-            service(part)
+    for part in every[1:]:
+        second_service(part)
+    for part in every:
+        last_service(part)
+    for part in every:
+        await_features(part)
 
     def hid_core(index):
         return remote(
@@ -507,12 +534,17 @@
             def _():
                 hid_sum[:, lanes] = total
 
+    hid_store = pltpu.make_async_copy(hid_ref, hid_any, load_sem.at[2])
+    kl_store = pltpu.make_async_copy(kl_ref, kl_any, load_sem.at[3])
+    kl_store.start()
+
     def hid_finish():
         total = hid_sum[...]
         for index in range(chips - 1):
             hid_far(index).wait_recv()
             total = total + hid_far_in[index].astype(f32)
         hid_ref[...] = total.astype(bf16)
+        hid_store.start()
         for step in range(chips):
             hid_core(step).wait_send()
         for index in range(chips - 1):
@@ -592,17 +624,20 @@
         block[...] += incoming[slot, :, columns_of(chunk)].astype(f32)
 
     def settle(chunk):
-        student[0:rows, grad_columns(side, chunk)] = block[
-            pl.ds(pl.multiple_of(side * rows, rows), rows), :
-        ]
         pair_out[:, columns_of(chunk)] = block[
             pl.ds(pl.multiple_of((PAIR - 1 - side) * rows, rows), rows), :
         ].astype(bf16)
         last_copy(chunk).start()
-
-    def result_copy(which, chunk):
-        spot = grad_columns(jnp.where(which == 0, side, PAIR - 1 - side), chunk)
-        return pltpu.make_async_copy(student.at[0:rows, spot], out_ref.at[:, spot], out_sem.at[which, chunk])
+        student[0:rows, columns_of(chunk)] = block[pl.ds(pl.multiple_of(side * rows, rows), rows), :]
+        own_store(chunk).start()
+
+    def own_store(chunk):
+        spot = columns_of(chunk)
+        return pltpu.make_async_copy(student.at[0:rows, spot], own_any.at[:, spot], out_sem.at[0, chunk])
+
+    def pair_store(chunk):
+        spot = columns_of(chunk)
+        return pltpu.make_async_copy(pair_in.at[:, spot], pair_any.at[:, spot], out_sem.at[1, chunk])
 
     def early_sums(chunk):
         @pl.loop(0, line - 2)
@@ -657,13 +692,17 @@
             def _():
                 for which in range(2):
                     feature_z(which, part).wait_send()
+                if part == 0:
+                    for step in range(1, chips):
+                        feature_z_far(step).wait_send()
 
             @pl.when(is_next)
             def _():
                 for which in (2, 3):
                     feature_core(which, 0, part).wait_send()
                     for step in range(1, chips):
-                        feature_x(which, step, part).wait_send()
+                        if which == 2 or part > 0:
+                            feature_x(which, step, part).wait_send()
                         feature_core(which, step, part).wait_send()
 
         @pl.loop(0, chunks)
@@ -694,12 +733,10 @@
         def _():
             for part in range(plan.halves):
                 y_copy(part, step).wait_recv()
+                pl.when(is_end)(end_pair(part, step).start)
 
             @pl.when(is_end)
             def _():
-                for part in range(plan.halves):
-                    end_pair(part, step).start()
-
                 @pl.when(step + plan.ahead < chunks)
                 def _():
                     for part in range(plan.halves):
@@ -734,9 +771,7 @@
         def _():
             chunk = step - plan.last_lag
             last_copy(chunk).wait_recv()
-            student[0:rows, grad_columns(PAIR - 1 - side, chunk)] = pair_in[:, columns_of(chunk)].astype(f32)
-            result_copy(0, chunk).start()
-            result_copy(1, chunk).start()
+            pair_store(chunk).start()
 
     @pl.loop(min(chunks + plan.last_lag, plan.hid_blocks), plan.hid_blocks)
     def _(index):
@@ -745,11 +780,14 @@
     if plan.hid_blocks >= chunks + plan.last_lag:
         hid_finish()
 
+    hid_store.wait()
+    kl_store.wait()
+
     @pl.loop(0, chunks)
     def _(chunk):
         last_copy(chunk).wait_send()
-        result_copy(0, chunk).wait()
-        result_copy(1, chunk).wait()
+        own_store(chunk).wait()
+        pair_store(chunk).wait()
 
     @pl.when(jnp.logical_not(is_end))
     def _():
@@ -764,6 +802,55 @@
                 line_copy(chunk, part, 0, up).wait_send()
 
 
+def place_results(
+    pieces,
+    kl_any, hid_any, own_any, pair_any, kl_out, hid_out, out_ref,
+    kl, hid, own, pair, wide, small_sem, big_sem,
+):
+    side = lax.axis_index("dp") % PAIR
+    rows, half = own.shape
+    step = rows // pieces
+
+    def load(which, piece):
+        where = pl.ds(piece * step, step)
+        source, target = ((own_any, own), (pair_any, pair))[which]
+        return pltpu.make_async_copy(source.at[where, :], target.at[where, :], big_sem.at[0, which, piece])
+
+    def store(which, piece):
+        where = pl.ds(piece * step, step)
+        first = (side if which == 0 else PAIR - 1 - side) * half
+        return pltpu.make_async_copy(
+            (own, wide)[which].at[where, :],
+            out_ref.at[where, pl.ds(pl.multiple_of(first, half), half)],
+            big_sem.at[1, which, piece],
+        )
+
+    small = [
+        [pltpu.make_async_copy(kl_any, kl, small_sem.at[0, 0]), pltpu.make_async_copy(kl, kl_out, small_sem.at[1, 0])],
+        [pltpu.make_async_copy(hid_any, hid, small_sem.at[0, 1]), pltpu.make_async_copy(hid, hid_out, small_sem.at[1, 1])],
+    ]
+    for piece in range(pieces):
+        for which in (1, 0):
+            load(which, piece).start()
+    for come, _ in small:
+        come.start()
+    for piece in range(pieces):
+        load(1, piece).wait()
+        where = pl.ds(piece * step, step)
+        wide[where, :] = pair[where, :].astype(f32)
+        store(1, piece).start()
+        load(0, piece).wait()
+        store(0, piece).start()
+    for come, leave in small:
+        come.wait()
+        leave.start()
+    for piece in range(pieces):
+        for which in range(2):
+            store(which, piece).wait()
+    for _, leave in small:
+        leave.wait()
+
+
 def per_device(shards, vocab, hidden_states, teacher_logits, head_weight):
     tokens, shard = hidden_states.shape
     model_width, columns = head_weight.shape
@@ -771,17 +858,19 @@
     dma = pltpu.SemaphoreType.DMA
     chips, halves, chunks = plan.chips, plan.halves, plan.chunks
     any_space = pl.BlockSpec(memory_space=pl.ANY)
-    in_vmem = pl.BlockSpec(memory_space=pltpu.VMEM)
-    divergence, hidden_grad, head_grad = pl.pallas_call(
+    divergence, hidden_grad, own_grad, pair_grad = pl.pallas_call(
         functools.partial(fused_kernel, plan),
         out_shape=(
             jax.ShapeDtypeStruct((1, tokens), f32),
             jax.ShapeDtypeStruct((tokens, shard), bf16),
-            jax.ShapeDtypeStruct((plan.rows, columns), f32),
+            jax.ShapeDtypeStruct((plan.rows, plan.half), f32),
+            jax.ShapeDtypeStruct((plan.rows, plan.half), bf16),
         ),
         in_specs=[any_space] * 3,
-        out_specs=(in_vmem, in_vmem, any_space),
+        out_specs=(any_space,) * 4,
         scratch_shapes=[
+            pltpu.VMEM((1, tokens), f32),
+            pltpu.VMEM((tokens, shard), bf16),
             pltpu.VMEM((model_width, columns), bf16),
             pltpu.VMEM((tokens, columns), f32),
             pltpu.VMEM((tokens, columns), bf16),
@@ -802,10 +891,11 @@
             pltpu.VMEM((tokens, LANES), f32),
             pltpu.VMEM((3, tokens, LANES), f32),
             pltpu.VMEM((vocab, 8, tokens), f32),
-            dma((2,)), dma((chips, columns // plan.dot_width)), dma((2, chunks)),
+            dma((4,)), dma((chips, columns // plan.dot_width)), dma((2, chunks)),
             dma((2 * chips - 1, halves)), dma((2 * chips - 1, halves)),
             dma((chips, halves)), dma((chips, halves)),
             dma((2, halves)), dma((2, halves)),
+            dma((chips,)), dma((chips,)),
             dma((2, chips, halves)), dma((2, chips, halves)),
             dma((3, chips, halves)), dma((3, chips, halves)),
             dma((vocab, halves)), dma((vocab, halves)),
@@ -821,6 +911,26 @@
             collective_id=0, has_side_effects=True, vmem_limit_bytes=67043328
         ),
     )(hidden_states, teacher_logits, head_weight)
+    pieces = 4
+    divergence, hidden_grad, head_grad = pl.pallas_call(
+        functools.partial(place_results, pieces),
+        out_shape=(
+            jax.ShapeDtypeStruct((1, tokens), f32),
+            jax.ShapeDtypeStruct((tokens, shard), bf16),
+            jax.ShapeDtypeStruct((plan.rows, columns), f32),
+        ),
+        in_specs=[any_space] * 4,
+        out_specs=(any_space,) * 3,
+        scratch_shapes=[
+            pltpu.VMEM((1, tokens), f32),
+            pltpu.VMEM((tokens, shard), bf16),
+            pltpu.VMEM((plan.rows, plan.half), f32),
+            pltpu.VMEM((plan.rows, plan.half), bf16),
+            pltpu.VMEM((plan.rows, plan.half), f32),
+            dma((2, 2)), dma((2, 2, pieces)),
+        ],
+        compiler_params=pltpu.CompilerParams(vmem_limit_bytes=16 * 1024 * 1024),
+    )(divergence, hidden_grad, own_grad, pair_grad)
     return divergence.reshape(tokens), hidden_grad, head_grad
 
 

time: 161 us -> 155 us (0.963)
  local copies, waits for them, and re-layouts: 7.77 us -> 4.51 us
  Pallas kernels: 152 us -> 149 us
    pallas_call x1, Pallas kernels: 152 us -> 147 us  [per_device(): pl.pallas_call(functools.partial(fused_kernel, plan), out_shape=(jax.Shap...]
    unnamed x3 -> x8, local copies, waits for them, and re-layouts: 7.77 us -> 4.51 us
    pallas_call x0 -> x1, Pallas kernels: none -> 2.64 us  [per_device(): pl.pallas_call(functools.partial(place_results, pieces), out_shape=(jax.S...]
where the time goes in v3:
time: 155 us; the launch traced here: 154 us
  Pallas kernels  149 us (96%)
  local copies, waits for them, and re-layouts  4.51 us (3%)
    pallas_call x1, Pallas kernels, per_device(): pl.pallas_call(functools.partial(fused_kernel, plan), out_shape=(jax.Shap...  147 us
    unnamed x8, local copies, waits for them, and re-layouts  4.51 us

profile of v3, /device:TPU:0, one launch (start us, length us, event | category | flops | bytes accessed | tf_op | source)
XLA Modules:
  0.0 154.4 jit_solution(16844282065257603801)
XLA Ops:
  0.6 146.6 %shard_map.58 = (f32[1,512]{1,0:T(1,128)}, bf16[512,512]{1,0:T(8,128)(2,1)}, f32[256,2048]{1,0:T(8,128)}, bf16[256,2048]{1,0:T(8,128)(2,1)}) custom-call(bf16[512,512]{1,0:T(8,128)(2,1)} %hidden_ref.1, bf16[512,4096]{1,0:T(8,128)(2,1)} %teacher_ref.1, bf16[2048,4096]{1,0:T(8,128)(2,1)} %weight_ref.1), custom_call_target="tpu_custom_call" | custom-call | tf_op jit(solution)/shard_map/pallas_call | solution.py:861
  147.3 0.0 copy-start
  147.3 1.6 %copy-done = f32[256,2048]{1,0:T(8,128)S(1)} copy-done((f32[256,2048]{1,0:T(8,128)S(1)}, f32[256,2048]{1,0:T(8,128)}, u32[]{:S(2)}) %copy-start) | copy-done | bytes 2097176
  148.8 0.0 copy-start.1
  148.8 1.2 copy-done.1
  150.1 0.0 copy-start.2
  150.1 1.0 copy-done.2
  151.1 0.0 copy-start.3
  151.1 0.7 copy-done.3
  151.8 2.6 %shard_map.59 = (f32[1,512]{1,0:T(1,128)}, bf16[512,512]{1,0:T(8,128)(2,1)}, f32[256,4096]{1,0:T(8,128)}) custom-call(f32[1,512]{1,0:T(1,128)S(1)} %copy-done.3, bf16[512,512]{1,0:T(8,128)(2,1)S(1)} %copy-done.2, f32[256,2048]{1,0:T(8,128)S(1)} %copy-done, bf16[256,2048]{1,0:T(8,128)(2,1)S(1)} %copy-done.1), custom_call_target="tpu_custom_call" | custom-call | tf_op jit(solution)/shard_map/pallas_call | solution.py:915
Async XLA Ops:
  147.3 1.6 %copy-start = (f32[256,2048]{1,0:T(8,128)S(1)}, f32[256,2048]{1,0:T(8,128)}, u32[]{:S(2)}) copy-start(f32[256,2048]{1,0:T(8,128)} %get-tuple-element.12.own_any) | copy-start | bytes 6291460
  148.8 1.2 copy-start.1
  150.1 1.0 copy-start.2
  151.1 0.7 copy-start.3

commit v4 on v3

--- a/solution.py
+++ b/solution.py
@@ -39,8 +39,8 @@
         self.lag = 2
         self.end_lag = self.lag + 2
         self.last_lag = max(self.end_lag + 1, self.chunks // 2 + 2)
-        self.ahead = 2
-        self.first = 2
+        self.ahead = 1
+        self.first = 1
         self.hid_width = min(256, shard)
         self.hid_subs = shard // self.hid_width
         self.hid_blocks = vocab * self.hid_subs
@@ -718,15 +718,30 @@
                     end_own(part, chunk).wait_send()
                     end_pair(part, chunk).wait_send()
 
+    def drain_sums():
+        kl_store.wait()
+        if plan.hid_blocks < chunks + plan.last_lag:
+            hid_store.wait()
+
+        @pl.when(jnp.logical_not(is_end))
+        def _():
+            @pl.loop(chunks - plan.window, chunks)
+            def _(chunk):
+                @pl.loop(0, place)
+                def _(part):
+                    line_copy(chunk, part, 0, down).wait_send()
+
+                @pl.loop(place + 1, line)
+                def _(part):
+                    line_copy(chunk, part, 0, up).wait_send()
+
+    def settled(chunk):
+        last_copy(chunk).wait_send()
+        own_store(chunk).wait()
+        pair_store(chunk).wait()
+
     @pl.loop(0, chunks + plan.last_lag)
     def _(step):
-        @pl.when(step < plan.hid_blocks)
-        def _():
-            hid_block(step)
-
-        if plan.hid_blocks < chunks + plan.last_lag:
-            pl.when(step == max(plan.hid_blocks, chunks))(hid_finish)
-
         pl.when(step == chunks + plan.lag - 1)(drain)
 
         @pl.when(step < chunks)
@@ -758,6 +773,13 @@
         def _():
             late_sums(step - plan.lag)
 
+        @pl.when(step < plan.hid_blocks)
+        def _():
+            hid_block(step)
+
+        if plan.hid_blocks < chunks + plan.last_lag:
+            pl.when(step == max(plan.hid_blocks, chunks))(hid_finish)
+
         @pl.when(
             jnp.logical_and(is_end, jnp.logical_and(step >= plan.end_lag, step < chunks + plan.end_lag))
         )
@@ -767,39 +789,27 @@
             add_incoming(chunk, 0)
             settle(chunk)
 
+        pl.when(step == chunks + plan.last_lag - 1)(drain_sums)
+
         @pl.when(step >= plan.last_lag)
         def _():
             chunk = step - plan.last_lag
             last_copy(chunk).wait_recv()
             pair_store(chunk).start()
 
+            @pl.when(chunk > 0)
+            def _():
+                settled(chunk - 1)
+
     @pl.loop(min(chunks + plan.last_lag, plan.hid_blocks), plan.hid_blocks)
     def _(index):
         hid_block(index)
 
     if plan.hid_blocks >= chunks + plan.last_lag:
         hid_finish()
-
-    hid_store.wait()
-    kl_store.wait()
-
-    @pl.loop(0, chunks)
-    def _(chunk):
-        last_copy(chunk).wait_send()
-        own_store(chunk).wait()
-        pair_store(chunk).wait()
-
-    @pl.when(jnp.logical_not(is_end))
-    def _():
-        @pl.loop(chunks - plan.window, chunks)
-        def _(chunk):
-            @pl.loop(0, place)
-            def _(part):
-                line_copy(chunk, part, 0, down).wait_send()
-
-            @pl.loop(place + 1, line)
-            def _(part):
-                line_copy(chunk, part, 0, up).wait_send()
+        hid_store.wait()
+
+    settled(chunks - 1)
 
 
 def place_results(
@@ -929,7 +939,7 @@
             pltpu.VMEM((plan.rows, plan.half), f32),
             dma((2, 2)), dma((2, 2, pieces)),
         ],
-        compiler_params=pltpu.CompilerParams(vmem_limit_bytes=16 * 1024 * 1024),
+        compiler_params=pltpu.CompilerParams(vmem_limit_bytes=67043328),
     )(divergence, hidden_grad, own_grad, pair_grad)
     return divergence.reshape(tokens), hidden_grad, head_grad
 

time: 155 us -> 148 us (0.955)
  local copies, waits for them, and re-layouts: 4.51 us -> 0 us
  Pallas kernels: 149 us -> 147 us
    unnamed x8 -> x0, local copies, waits for them, and re-layouts: 4.51 us -> none
    pallas_call x1, Pallas kernels: 147 us -> 144 us  [per_device(): pl.pallas_call(functools.partial(fused_kernel, plan), out_shape=(jax.Shap...]
where the time goes in v4:
time: 148 us; the launch traced here: 147 us
  Pallas kernels  147 us (99%)
    pallas_call x1, Pallas kernels, per_device(): pl.pallas_call(functools.partial(fused_kernel, plan), out_shape=(jax.Shap...  144 us
    pallas_call x1, Pallas kernels, per_device(): pl.pallas_call(functools.partial(place_results, pieces), out_shape=(jax.S...  3.34 us

profile of v4, /device:TPU:0, one launch (start us, length us, event | category | flops | bytes accessed | tf_op | source)
XLA Modules:
  0.0 147.5 jit_solution(11249678913716786431)
XLA Ops:
  0.6 143.5 %shard_map.58 = (f32[1,512]{1,0:T(1,128)}, bf16[512,512]{1,0:T(8,128)(2,1)}, f32[256,2048]{1,0:T(8,128)}, bf16[256,2048]{1,0:T(8,128)(2,1)}) custom-call(bf16[512,512]{1,0:T(8,128)(2,1)} %hidden_ref.1, bf16[512,4096]{1,0:T(8,128)(2,1)} %teacher_ref.1, bf16[2048,4096]{1,0:T(8,128)(2,1)} %weight_ref.1), custom_call_target="tpu_custom_call" | custom-call | tf_op jit(solution)/shard_map/pallas_call | solution.py:871
  144.2 3.3 %shard_map.59 = (f32[1,512]{1,0:T(1,128)}, bf16[512,512]{1,0:T(8,128)(2,1)}, f32[256,4096]{1,0:T(8,128)}) custom-call(f32[1,512]{1,0:T(1,128)} %get-tuple-element.10.kl_any, bf16[512,512]{1,0:T(8,128)(2,1)} %get-tuple-element.11.hid_any, f32[256,2048]{1,0:T(8,128)} %get-tuple-element.12.own_any, bf16[256,2048]{1,0:T(8,128)(2,1)} %get-tuple-element.13.pair_any), custom_call_target="tpu_custom_call" | custom-call | tf_op jit(solution)/shard_map/pallas_call | solution.py:925

commit v5 on v4

--- a/solution.py
+++ b/solution.py
@@ -35,7 +35,7 @@
         self.rows2 = model_width // self.line
         self.rows = self.rows2 // PAIR
         self.window = min(6, self.chunks)
-        self.dot_width = min(512, columns)
+        self.dot_width = min(1024, columns)
         self.lag = 2
         self.end_lag = self.lag + 2
         self.last_lag = max(self.end_lag + 1, self.chunks // 2 + 2)
@@ -44,6 +44,7 @@
         self.hid_width = min(256, shard)
         self.hid_subs = shard // self.hid_width
         self.hid_blocks = vocab * self.hid_subs
+        self.store_lag = min(8, self.chunks)
         self.slots = 2 if self.line == 4 else self.line + 1
 
 
@@ -580,7 +581,7 @@
         return remote(
             outgoing.at[lax.rem(chunk, plan.window), part],
             incoming.at[slot, :, columns_of(chunk)],
-            line_send.at[part, chunk], line_recv.at[slot, chunk], dp=target,
+            line_send.at[part, lax.rem(chunk, plan.window)], line_recv.at[slot, chunk], dp=target,
         )
 
     def send_sum(chunk, part, target, slot, source):
@@ -738,7 +739,6 @@
     def settled(chunk):
         last_copy(chunk).wait_send()
         own_store(chunk).wait()
-        pair_store(chunk).wait()
 
     @pl.loop(0, chunks + plan.last_lag)
     def _(step):
@@ -801,6 +801,10 @@
             def _():
                 settled(chunk - 1)
 
+            @pl.when(chunk >= plan.store_lag)
+            def _():
+                pair_store(chunk - plan.store_lag).wait()
+
     @pl.loop(min(chunks + plan.last_lag, plan.hid_blocks), plan.hid_blocks)
     def _(index):
         hid_block(index)
@@ -810,6 +814,10 @@
         hid_store.wait()
 
     settled(chunks - 1)
+
+    @pl.loop(chunks - plan.store_lag, chunks)
+    def _(chunk):
+        pair_store(chunk).wait()
 
 
 def place_results(
@@ -912,7 +920,7 @@
             dma((halves, chunks)), dma((halves, chunks)),
             dma((halves, chunks)), dma((halves, chunks)),
             dma((halves, chunks)), dma((halves, chunks)),
-            dma((plan.line, chunks)), dma((plan.slots, chunks)),
+            dma((plan.line, plan.window)), dma((plan.slots, chunks)),
             dma((chunks,)), dma((chunks,)),
             dma((chips,)), dma((chips,)),
             dma((chips - 1,)), dma((chips - 1,)),

time: 148 us -> 147 us (level)
  no operation moved by 1% of the time
where the time goes in v5:
time: 147 us
  Pallas kernels  146 us (99%)
    pallas_call x1, Pallas kernels, per_device(): pl.pallas_call(functools.partial(fused_kernel, plan), out_shape=(jax.Shap...  143 us
    pallas_call x1, Pallas kernels, per_device(): pl.pallas_call(functools.partial(place_results, pieces), out_shape=(jax.S...  3.34 us

profile of v5, /device:TPU:0, one launch (start us, length us, event | category | flops | bytes accessed | tf_op | source)
XLA Modules:
  0.0 147.1 jit_solution(13222214891500732177)
XLA Ops:
  0.6 143.1 %shard_map.58 = (f32[1,512]{1,0:T(1,128)}, bf16[512,512]{1,0:T(8,128)(2,1)}, f32[256,2048]{1,0:T(8,128)}, bf16[256,2048]{1,0:T(8,128)(2,1)}) custom-call(bf16[512,512]{1,0:T(8,128)(2,1)} %hidden_ref.1, bf16[512,4096]{1,0:T(8,128)(2,1)} %teacher_ref.1, bf16[2048,4096]{1,0:T(8,128)(2,1)} %weight_ref.1), custom_call_target="tpu_custom_call" | custom-call | tf_op jit(solution)/shard_map/pallas_call | solution.py:879
  143.7 3.3 %shard_map.59 = (f32[1,512]{1,0:T(1,128)}, bf16[512,512]{1,0:T(8,128)(2,1)}, f32[256,4096]{1,0:T(8,128)}) custom-call(f32[1,512]{1,0:T(1,128)} %get-tuple-element.10.kl_any, bf16[512,512]{1,0:T(8,128)(2,1)} %get-tuple-element.11.hid_any, f32[256,2048]{1,0:T(8,128)} %get-tuple-element.12.own_any, bf16[256,2048]{1,0:T(8,128)(2,1)} %get-tuple-element.13.pair_any), custom_call_target="tpu_custom_call" | custom-call | tf_op jit(solution)/shard_map/pallas_call | solution.py:933
